TPU v7x, 256 devices: a whole 4x4x8 slice. The times are simulated.
256 devices in a mesh: shadow: 32 (over z, y_lo, core), vocab: 8 (over y_hi, x).
Axes of the slice: x: 4, y: 4 (y_hi: 2, y_lo: 2; y = y_hi * 2 + y_lo), z: 8, core: 2. Of those that a mesh axis runs over, the one named last changes fastest.
Arguments:
- hidden: bfloat16 [128, 128, 2048], P('shadow'), may hold values from -18 to 18
- targets: int32 [128], replicated, may hold values from 0 to 32767
- membership: int32 [128, 4], P('shadow'), may hold values from 0 to 1, as said below
- unembedding: bfloat16 [32768, 2048], P(('shadow', 'vocab')), may hold values from -1 to 1
Outputs:
- score: float32 [128, 128], P('shadow', 'vocab')
Inputs may be any that keep to these rules, and one draw needn't show every extreme that they name: `membership`: each candidate sequence is a member of exactly 64 of the shadow models.
All inputs are finite; a program needn't handle non-finite values.
Results may differ from a plain program's by a relative error of at most 0.00055.
Values may be sent and summed in bfloat16 or wider, within the bound.
No kernel may reach another device: no remote copies, remote signals or barrier semaphores. Data moves between devices by JAX's collectives and lax.ppermute only.
A program may use at most 64 MiB of HBM per device.

v0:
```python
import functools

import jax
import jax.numpy as jnp
from jax import lax
from jax.experimental import pallas as pl
from jax.experimental.pallas import tpu as pltpu
from jax.sharding import Mesh, PartitionSpec as P


SEQ = 32


NEG_FILL = -1e30
VAR_FLOOR = 0.5
PARTS = 2


def around(size, step):
    return [(k, (k + step) % size) for k in range(size)]


def across_y():
    place = lambda y, core: (y % 2 * 2 + core) * 2 + y // 2
    return [(place(y, core), place((y + 2 * core - 1) % 4, core)) for y in range(4) for core in (0, 1)]


def scores_kernel(fresh_counts, held, blocks, places, *refs):
    refs = list(refs)
    first_ref, wanted_ref = refs.pop(0), refs.pop(0)
    stores = {b: refs.pop(0) for b in held}
    fresh_refs = {b: refs.pop(0) for b in fresh_counts}
    head_refs = [refs.pop(0) for _ in places]
    out = refs.pop(0)
    copies = {}
    if fresh_counts:
        stores[min(fresh_counts)], sems = refs
        for b, ref in fresh_refs.items():
            for half in range(2):
                tokens = pl.ds(64 * half, 64)
                copies[b, half] = pltpu.make_async_copy(
                    ref.at[:, tokens],
                    stores[b - b % 2].at[b % 2, :, tokens],
                    sems.at[len(copies)],
                )
        queue = list(copies.values())
        for copy in queue[:2]:
            copy.start()
        queue = queue[2:]
    groups, sizes = [[]], [0]
    for place, ref in zip(places, head_refs):
        if sizes[-1] + ref.shape[0] > 256:
            groups.append([])
            sizes.append(0)
        groups[-1].append((place, ref))
        sizes[-1] += ref.shape[0]
    for n, b in enumerate(blocks):
        for half in range(2):
            if copies:
                copies[b, half].wait()
                if queue:
                    queue.pop(0).start()
            rows = jnp.concatenate(
                [
                    stores[b - b % 2][b % 2, k, 16 * v : 16 * v + 16, :]
                    for v in range(4 * half, 4 * half + 4)
                    for k in range(4)
                ],
                axis=0,
            )
            lanes = slice(256 * half, 256 * half + 256)
            wanted = wanted_ref[0:1, lanes]
            pieces = []
            for group in groups:
                head = jnp.concatenate([ref[...] for _, ref in group], axis=0)
                logits = lax.dot_general(
                    head, rows, (((1,), (1,)), ((), ())), preferred_element_type=jnp.float32
                )
                at = 0
                for place, ref in group:
                    part = logits[at : at + ref.shape[0]]
                    at += ref.shape[0]
                    vocab_rows = lax.broadcasted_iota(jnp.int32, part.shape, 0) + first_ref[place]
                    pieces.append((part, vocab_rows == wanted))
            target_logit = sum(
                jnp.sum(jnp.where(hit, part, 0.0), axis=0, keepdims=True) for part, hit in pieces
            )
            others = [jnp.where(hit, NEG_FILL, part) for part, hit in pieces]
            highest = functools.reduce(
                jnp.maximum, [jnp.max(part, axis=0, keepdims=True) for part in others]
            )
            summed = sum(
                jnp.sum(jnp.exp(part - highest), axis=0, keepdims=True) for part in others
            )
            out[n, 0:1, lanes] = highest
            out[n, 1:2, lanes] = summed
            out[n, 2:3, lanes] = target_logit


def score_blocks(stores, fresh, blocks, pieces, first, wanted):
    heads = [head for head, _ in pieces]
    vmem = pl.BlockSpec(memory_space=pltpu.VMEM)
    head_rows = sum(head.shape[0] for head in heads)
    outs = [jax.ShapeDtypeStruct((len(blocks), 3, 512), jnp.float32)]
    if fresh:
        outs.append(jax.ShapeDtypeStruct((2, 4, 128, 2048), jnp.bfloat16))
    results = pl.pallas_call(
        functools.partial(
            scores_kernel, list(fresh), list(stores), blocks, [place for _, place in pieces]
        ),
        in_specs=[pl.BlockSpec(memory_space=pltpu.SMEM), vmem]
        + [vmem] * len(stores)
        + [pl.BlockSpec(memory_space=pltpu.HBM)] * len(fresh)
        + [vmem] * len(heads),
        out_specs=[vmem] * len(outs),
        out_shape=outs,
        scratch_shapes=[pltpu.SemaphoreType.DMA((4,))] if fresh else [],
        compiler_params=pltpu.CompilerParams(vmem_limit_bytes=12 << 20),
        cost_estimate=pl.CostEstimate(
            flops=2 * 512 * len(blocks) * head_rows * 2048,
            bytes_accessed=2 * 2048 * (head_rows + 512 * len(blocks)),
            transcendentals=512 * len(blocks) * head_rows,
        ),
    )(
        first,
        wanted,
        *stores.values(),
        *[pltpu.with_memory_space_constraint(rows, pltpu.HBM) for rows in fresh.values()],
        *heads,
    )
    return results


def wanted_kernel(targets_ref, wanted_ref):
    targets = jnp.broadcast_to(targets_ref[...], (8, 128))
    turned = [targets] + [pltpu.roll(targets, 16 * k, 1) for k in range(1, 8)]
    place = lax.broadcasted_iota(jnp.int32, (8, 128), 1) // 16
    for quarter in range(4):
        lanes = targets
        for s in range(8):
            lanes = jnp.where(place == s, turned[(s - 2 * quarter - s // 4) % 8], lanes)
        wanted_ref[0:1, 128 * quarter : 128 * quarter + 128] = lanes[0:1]


def wanted_rows(targets):
    vmem = pl.BlockSpec(memory_space=pltpu.VMEM)
    return pl.pallas_call(
        wanted_kernel,
        in_specs=[vmem],
        out_specs=vmem,
        out_shape=jax.ShapeDtypeStruct((1, 512), jnp.int32),
        compiler_params=pltpu.CompilerParams(vmem_limit_bytes=4 << 20),
    )(targets.reshape(1, 128))


def after(values, others):
    return lax.optimization_barrier((*values, *others))[: len(values)]


def combine(earlier, latter):
    raised = jnp.maximum(earlier[:, 0], latter[:, 0])
    summed = earlier[:, 1] * jnp.exp(earlier[:, 0] - raised) + latter[:, 1] * jnp.exp(
        latter[:, 0] - raised
    )
    return jnp.stack([raised, summed, earlier[:, 2] + latter[:, 2]], axis=1)


def per_device(hidden, targets, membership, unembedding):
    shadow_count, token_count, _ = hidden.shape
    head_rows = unembedding.shape[0]
    z, yl, core = lax.axis_index("z"), lax.axis_index("yl"), lax.axis_index("c")
    vocab_index = lax.axis_index(("yh", "x"))
    part_rows = head_rows // PARTS

    place = jnp.arange(8 * PARTS, dtype=jnp.int32)
    source = (((z - place // PARTS) & 7) * 4 + yl * 2 + core) * 8 + vocab_index
    first = source * head_rows + place % PARTS * part_rows

    swap = [(0, 1), (1, 0)]
    up = [unembedding[k * part_rows : (k + 1) * part_rows] for k in range(PARTS)]
    down = list(up)
    gathered = [[(unembedding, 0)]]

    def forward(step):
        for k in range(PARTS):
            up[k] = lax.ppermute(up[k], "z", around(8, 1))
            down[k] = lax.ppermute(down[k], "z", around(8, -1))
        gathered.append(
            [(up[k], PARTS * step + k) for k in range(PARTS)]
            + [(down[k], PARTS * (8 - step) + k) for k in range(PARTS)]
        )

    forward(1)
    beside = lax.ppermute(hidden, "c", swap)
    across = lax.ppermute(hidden, ("yl", "c", "yh"), across_y())
    wanted = wanted_rows(targets)
    forward(2)
    near_found, near = score_blocks({}, {0: hidden, 1: beside}, [0, 1], gathered[1], first, wanted)
    forward(3)
    diagonal = lax.ppermute(across, "c", swap)
    (latter,) = score_blocks({0: near}, {}, [0, 1], gathered[2], first, wanted)
    near_found = combine(near_found, latter)
    last = []
    for k in range(PARTS):
        if k < PARTS // 2:
            last.append((lax.ppermute(up[k], "z", around(8, 1)), PARTS * 4 + k))
        else:
            last.append((lax.ppermute(down[k], "z", around(8, -1)), PARTS * 4 + k))
    (wanted_far,) = after((wanted,), (near_found,))
    far_found, far = score_blocks(
        {}, {2: across, 3: diagonal}, [2, 3], gathered[1] + gathered[2], first, wanted_far
    )
    found = jnp.concatenate([near_found, far_found])
    stores, every = {0: near, 2: far}, [0, 1, 2, 3]
    (latter,) = score_blocks(stores, {}, every, gathered[3], first, wanted_far)
    found = combine(found, latter)
    (wanted_last,) = after((wanted,), (found,))
    (latter,) = score_blocks(stores, {}, every, gathered[0] + last, first, wanted_last)
    found = combine(found, latter)

    both = jnp.stack([found[:, 0] + jnp.log(found[:, 1]), found[:, 2]], axis=1)
    both = both.reshape(2, 2, 2, 8, 64)
    both = jnp.where(yl == 1, both[::-1], both)
    both = jnp.where(core == 1, both[:, ::-1], both)
    message = both.transpose(0, 1, 3, 2, 4).reshape(32, 1, 128)
    received = lax.all_to_all(
        message, ("yl", "c", "yh", "x"), split_axis=0, concat_axis=0, tiled=True
    ).reshape(32, 128)
    partial, target_logit = received[:, :64], jnp.sum(received[:, 64:], axis=0)
    highest = jnp.max(partial, axis=0)
    summed = jnp.sum(jnp.exp(partial - highest[None]), axis=0)
    slice_tokens = token_count // 8
    confidence = (target_logit - (highest + jnp.log(summed))).reshape(shadow_count, slice_tokens)

    member_tokens = jnp.repeat(membership, SEQ, axis=1)
    outside = (
        1 - lax.dynamic_slice_in_dim(member_tokens, vocab_index * slice_tokens, slice_tokens, 1)
    ).astype(jnp.float32)
    weighted = outside * confidence
    sums = jnp.concatenate([jnp.sum(weighted, axis=0), jnp.sum(weighted * confidence, axis=0)])
    copies = jnp.broadcast_to(sums, (32, 1, 2 * slice_tokens))
    total = jnp.sum(
        lax.all_to_all(copies, ("z", "yl", "c"), split_axis=0, concat_axis=0, tiled=True), axis=(0, 1)
    )
    first_moment, second_moment = total[:slice_tokens], total[slice_tokens:]
    out_count = 64 - outside
    out_mean = (first_moment[None, :] - weighted) / out_count
    out_variance = (
        second_moment[None, :] - weighted * confidence
    ) / out_count - out_mean * out_mean
    return (confidence - out_mean) * lax.rsqrt(jnp.maximum(out_variance, 0.0) + VAR_FLOOR)


def solution(mesh):
    parts = Mesh(mesh.devices.reshape(8, 2, 2, 2, 4), ("z", "yl", "c", "yh", "x"))
    shadow, vocab = ("z", "yl", "c"), ("yh", "x")

    return jax.shard_map(
        per_device,
        mesh=parts,
        in_specs=(P(shadow, None, None), P(), P(shadow, None), P(shadow + vocab, None)),
        out_specs=P(shadow, vocab),
        check_vma=False,
    )
```

profile of v0, /device:TPU:1, one launch (start us, length us, event | category | flops | bytes accessed | tf_op | source)
XLA Modules:
  0.0 124.5 jit_solution(59049126595612113)
XLA Ops:
  0.0 2.1 %collective-permute-start.9 = (bf16[4,128,2048]{2,1,0:T(8,128)(2,1)}, bf16[4,128,2048]{2,1,0:T(8,128)(2,1)}, u32[]{:S(2)}, u32[]{:S(2)}) collective-permute-start(bf16[4,128,2048]{2,1,0:T(8,128)(2,1)} %refs_2_.1), channel_id=1, source_target_pairs={{0,20},{8,24},{16,0},{24,12},{4,16},{12,28},{20,4},{28,8},{1,21},{... | collective-permute-start | bytes 6291464 | tf_op jit(solution)/shard_map/ppermute | solution.py:195
  2.1 2.4 %collective-permute-start = (bf16[4,128,2048]{2,1,0:T(8,128)(2,1)}, bf16[4,128,2048]{2,1,0:T(8,128)(2,1)}, u32[]{:S(2)}, u32[]{:S(2)}) collective-permute-start(bf16[4,128,2048]{2,1,0:T(8,128)(2,1)} %refs_2_.1), channel_id=1, source_target_pairs={{0,8},{8,0},{1,9},{9,1},{2,10},{10,2},{3,11},{11,3},{4,12},{12,4},... | collective-permute-start | bytes 6291464 | tf_op jit(solution)/shard_map/ppermute | solution.py:194
  4.5 22.8 %collective-permute-done.9.refs_2_ = bf16[4,128,2048]{2,1,0:T(8,128)(2,1)} collective-permute-done((bf16[4,128,2048]{2,1,0:T(8,128)(2,1)}, bf16[4,128,2048]{2,1,0:T(8,128)(2,1)}, u32[]{:S(2)}, u32[]{:S(2)}) %collective-permute-start.9) | collective-permute-done | bytes 2097184 | tf_op jit(solution)/shard_map/ppermute | solution.py:195
  27.3 2.3 %collective-permute-start.10 = (bf16[4,128,2048]{2,1,0:T(8,128)(2,1)}, bf16[4,128,2048]{2,1,0:T(8,128)(2,1)}, u32[]{:S(2)}, u32[]{:S(2)}) collective-permute-start(bf16[4,128,2048]{2,1,0:T(8,128)(2,1)} %collective-permute-done.9.refs_2_), channel_id=1, source_target_pairs={{0,8},{8,0},{1,9},{9,1},{2,10},{10,2},{3,11},{11,3},{4,12},{12,4},... | collective-permute-start | bytes 6291464 | tf_op jit(solution)/shard_map/ppermute | solution.py:200
  29.6 1.1 fusion.21
  30.6 4.5 %collective-permute-start.4 = (bf16[64,2048]{1,0:T(8,128)(2,1)S(1)}, bf16[64,2048]{1,0:T(8,128)(2,1)S(1)}, u32[]{:S(2)}, u32[]{:S(2)}) collective-permute-start(bf16[64,2048]{1,0:T(8,128)(2,1)S(1)} %get-tuple-element.23), channel_id=1, source_target_pairs={{0,224},{32,0},{64,32},{96,64},{128,96},{160,128},{192,160},{224,1... | collective-permute-start | bytes 786440 | tf_op jit(solution)/shard_map/ppermute | solution.py:187
  35.1 2.7 %collective-permute-start.3 = (bf16[64,2048]{1,0:T(8,128)(2,1)S(1)}, bf16[64,2048]{1,0:T(8,128)(2,1)S(1)}, u32[]{:S(2)}, u32[]{:S(2)}) collective-permute-start(bf16[64,2048]{1,0:T(8,128)(2,1)S(1)} %get-tuple-element.24), channel_id=1, source_target_pairs={{0,224},{32,0},{64,32},{96,64},{128,96},{160,128},{192,160},{224,1... | collective-permute-start | bytes 786440 | tf_op jit(solution)/shard_map/ppermute | solution.py:187
  37.8 3.0 %collective-permute-done.4.refs_7_ = bf16[64,2048]{1,0:T(8,128)(2,1)S(1)} collective-permute-done((bf16[64,2048]{1,0:T(8,128)(2,1)S(1)}, bf16[64,2048]{1,0:T(8,128)(2,1)S(1)}, u32[]{:S(2)}, u32[]{:S(2)}) %collective-permute-start.4) | collective-permute-done | bytes 262176 | tf_op jit(solution)/shard_map/ppermute | solution.py:187
  40.8 3.1 %collective-permute-done.2.refs_5_ = bf16[64,2048]{1,0:T(8,128)(2,1)S(1)} collective-permute-done((bf16[64,2048]{1,0:T(8,128)(2,1)S(1)}, bf16[64,2048]{1,0:T(8,128)(2,1)S(1)}, u32[]{:S(2)}, u32[]{:S(2)}) %collective-permute-start.2) | collective-permute-done | bytes 262176 | tf_op jit(solution)/shard_map/ppermute | solution.py:186
  43.9 0.3 collective-permute-start.8
  44.2 2.2 %collective-permute-done.3.refs_6_ = bf16[64,2048]{1,0:T(8,128)(2,1)S(1)} collective-permute-done((bf16[64,2048]{1,0:T(8,128)(2,1)S(1)}, bf16[64,2048]{1,0:T(8,128)(2,1)S(1)}, u32[]{:S(2)}, u32[]{:S(2)}) %collective-permute-start.3) | collective-permute-done | bytes 262176 | tf_op jit(solution)/shard_map/ppermute | solution.py:187
  46.4 0.0 collective-permute-start.6
  46.4 3.1 %collective-permute-done.1.refs_4_ = bf16[64,2048]{1,0:T(8,128)(2,1)S(1)} collective-permute-done((bf16[64,2048]{1,0:T(8,128)(2,1)S(1)}, bf16[64,2048]{1,0:T(8,128)(2,1)S(1)}, u32[]{:S(2)}, u32[]{:S(2)}) %collective-permute-start.1) | collective-permute-done | bytes 262176 | tf_op jit(solution)/shard_map/ppermute | solution.py:186
  49.5 2.5 %collective-permute-done.8.refs_6_.refs_11_ = bf16[64,2048]{1,0:T(8,128)(2,1)S(1)} collective-permute-done((bf16[64,2048]{1,0:T(8,128)(2,1)S(1)}, bf16[64,2048]{1,0:T(8,128)(2,1)S(1)}, u32[]{:S(2)}, u32[]{:S(2)}) %collective-permute-start.8) | collective-permute-done | bytes 262176 | tf_op jit(solution)/shard_map/ppermute | solution.py:187
  52.0 3.4 %collective-permute-start.7 = (bf16[64,2048]{1,0:T(8,128)(2,1)S(1)}, bf16[64,2048]{1,0:T(8,128)(2,1)S(1)}, u32[]{:S(2)}, u32[]{:S(2)}) collective-permute-start(bf16[64,2048]{1,0:T(8,128)(2,1)S(1)} %collective-permute-done.3.refs_6_), channel_id=1, source_target_pairs={{0,224},{32,0},{64,32},{96,64},{128,96},{160,128},{192,160},{224,1... | collective-permute-start | bytes 786440 | tf_op jit(solution)/shard_map/ppermute | solution.py:187
  55.4 0.9 collective-permute-start.14
  56.3 4.4 %collective-permute-done.5.refs_3_.refs_8_ = bf16[64,2048]{1,0:T(8,128)(2,1)S(1)} collective-permute-done((bf16[64,2048]{1,0:T(8,128)(2,1)S(1)}, bf16[64,2048]{1,0:T(8,128)(2,1)S(1)}, u32[]{:S(2)}, u32[]{:S(2)}) %collective-permute-start.5) | collective-permute-done | bytes 262176 | tf_op jit(solution)/shard_map/ppermute | solution.py:186
  60.8 0.0 collective-permute-start.11
  60.8 0.7 copy-done.1
  61.4 0.1 shard_map.46.refs_1_
  61.5 0.0 collective-permute-done.7.refs_5_.refs_10_
  61.5 0.1 collective-permute-start.12
  61.6 4.2 %collective-permute-done.14.refs_7_ = bf16[64,2048]{1,0:T(8,128)(2,1)S(1)} collective-permute-done((bf16[64,2048]{1,0:T(8,128)(2,1)S(1)}, bf16[64,2048]{1,0:T(8,128)(2,1)S(1)}, u32[]{:S(2)}, u32[]{:S(2)}) %collective-permute-start.14) | collective-permute-done | bytes 262176 | tf_op jit(solution)/shard_map/ppermute | solution.py:187
  65.8 3.4 %collective-permute-start.13 = (bf16[64,2048]{1,0:T(8,128)(2,1)S(1)}, bf16[64,2048]{1,0:T(8,128)(2,1)S(1)}, u32[]{:S(2)}, u32[]{:S(2)}) collective-permute-start(bf16[64,2048]{1,0:T(8,128)(2,1)S(1)} %collective-permute-done.7.refs_5_.refs_10_), channel_id=1, source_target_pairs={{0,224},{32,0},{64,32},{96,64},{128,96},{160,128},{192,160},{224,1... | collective-permute-start | bytes 786440 | tf_op jit(solution)/shard_map/ppermute | solution.py:187
  69.2 0.0 collective-permute-start.16
  69.3 1.4 %collective-permute-start.15 = (bf16[64,2048]{1,0:T(8,128)(2,1)S(1)}, bf16[64,2048]{1,0:T(8,128)(2,1)S(1)}, u32[]{:S(2)}, u32[]{:S(2)}) collective-permute-start(bf16[64,2048]{1,0:T(8,128)(2,1)S(1)} %collective-permute-done.11.refs_4_), channel_id=1, source_target_pairs={{0,32},{32,64},{64,96},{96,128},{128,160},{160,192},{192,224},{224... | collective-permute-start | bytes 786440 | tf_op jit(solution)/shard_map/ppermute | solution.py:206
  70.7 5.0 %shard_map.47 = (f32[2,3,512]{2,1,0:T(4,128)S(1)}, bf16[2,4,128,2048]{3,2,1,0:T(8,128)(2,1)S(1)}) custom-call(s32[16]{0:T(128)S(1)} %fusion.12.refs_0_, s32[1,512]{1,0:T(1,128)S(1)} %shard_map.46.refs_1_, bf16[4,128,2048]{2,1,0:T(8,128)(2,1)} %refs_2_.1, bf16[4,128,2048]{2,1,0:T(8,128)(2,1)} %collective-permute-done.refs_3_, ...), custom_call_target="tpu_custom_call" | custom-call | flops 1073741824 | bytes 5242880 | tf_op jit(solution)/shard_map/pallas_call | solution.py:107
  75.7 2.1 %shard_map.48 = f32[2,3,512]{2,1,0:T(4,128)S(1)} custom-call(s32[16]{0:T(128)S(1)} %fusion.12.refs_0_, s32[1,512]{1,0:T(1,128)S(1)} %shard_map.46.refs_1_, bf16[2,4,128,2048]{3,2,1,0:T(8,128)(2,1)S(1)} %get-tuple-element.11.refs_2_, bf16[64,2048]{1,0:T(8,128)(2,1)S(1)} %collective-permute-done.5.refs_3_.refs_8_, ...), custom_call_target="tpu_custom_call" | custom-call | flops 1073741824 | bytes 5242880 | tf_op jit(solution)/shard_map/pallas_call | solution.py:107
  77.9 5.4 %shard_map.49 = (f32[2,3,512]{2,1,0:T(4,128)S(1)}, bf16[2,4,128,2048]{3,2,1,0:T(8,128)(2,1)S(1)}) custom-call(s32[16]{0:T(128)S(1)} %fusion.12.refs_0_, s32[1,512]{1,0:T(1,128)S(1)} %shard_map.46.refs_1_, bf16[4,128,2048]{2,1,0:T(8,128)(2,1)} %collective-permute-done.9.refs_2_, bf16[4,128,2048]{2,1,0:T(8,128)(2,1)} %collective-permute-done.10.refs_3_, ...), custom_call_target="tpu_custom_call" | custom-call | flops 2147483648 | bytes 6291456 | tf_op jit(solution)/shard_map/pallas_call | solution.py:107
  83.3 0.0 copy-start
  83.3 3.6 %shard_map.50 = f32[4,3,512]{2,1,0:T(4,128)S(1)} custom-call(s32[16]{0:T(128)S(1)} %fusion.12.refs_0_, s32[1,512]{1,0:T(1,128)S(1)} %shard_map.46.refs_1_, bf16[2,4,128,2048]{3,2,1,0:T(8,128)(2,1)S(1)} %get-tuple-element.11.refs_2_, bf16[2,4,128,2048]{3,2,1,0:T(8,128)(2,1)S(1)} %get-tuple-element.14.refs_3_, ...), custom_call_target="tpu_custom_call" | custom-call | flops 2147483648 | bytes 9437184 | tf_op jit(solution)/shard_map/pallas_call | solution.py:107
  86.8 0.0 copy-start.2
  86.9 3.5 %shard_map.51 = f32[4,3,512]{2,1,0:T(4,128)S(1)} custom-call(s32[16]{0:T(128)S(1)} %fusion.12.refs_0_, s32[1,512]{1,0:T(1,128)S(1)} %shard_map.46.refs_1_, bf16[2,4,128,2048]{3,2,1,0:T(8,128)(2,1)S(1)} %get-tuple-element.11.refs_2_, bf16[2,4,128,2048]{3,2,1,0:T(8,128)(2,1)S(1)} %get-tuple-element.14.refs_3_, bf16[128,2048]{1,0:T(8,128)(2,1)S(1)} %copy-done, ...), custom_call_target="tpu_custom_call" | custom-call | flops 2147483648 | bytes 9437184 | tf_op jit(solution)/shard_map/pallas_call | solution.py:107
  90.4 0.2 add_reduce_fusion
  90.5 0.1 stack.9
  90.6 0.1 stack.10
  90.8 0.7 reshape.26
  91.5 12.0 %all-to-all-start = ((f32[32,1,128]{2,1,0:T(1,128)}), f32[32,1,128]{2,1,0:T(1,128)S(1)}, u32[]{:S(2)}, u32[]{:S(2)}) async-start(f32[32,1,128]{2,1,0:T(1,128)} %bitcast.4), calls=%async_computation | async-start | bytes 32768 | tf_op jit(solution)/shard_map/all_to_all | solution.py:226
  103.4 0.1 broadcast_in_dim.4
  103.5 0.1 reshape.28
  103.6 6.8 %all-to-all-done = f32[32,1,128]{2,1,0:T(1,128)S(1)} async-done(((f32[32,1,128]{2,1,0:T(1,128)}), f32[32,1,128]{2,1,0:T(1,128)S(1)}, u32[]{:S(2)}, u32[]{:S(2)}) %all-to-all-start) | async-done | bytes 16416 | tf_op jit(solution)/shard_map/all_to_all | solution.py:226
  110.4 0.1 exponential_reduce_fusion
  110.5 0.1 sub.95
  110.5 0.1 fusion.9
  110.6 0.1 pad_maximum_fusion.5
  110.7 12.9 %all_to_all.10 = f32[32,1,32]{2,1,0:T(1,128)S(1)} all-to-all(f32[32,1,32]{2,1,0:T(1,128)S(1)} %broadcast_in_dim.10), channel_id=1, replica_groups=mesh['z'=8,'yl'=2,'c'=2,'yh'=2,'x'=4] {'z','yl','c'}, dimensions={0} | all-to-all | bytes 8192 | tf_op jit(solution)/shard_map/all_to_all | solution.py:243
  123.7 0.1 fusion.22
  123.8 0.7 rsqrt_multiply_fusion
  (23 shorter events, 0.2 us)
Async XLA Ops:
  0.0 27.3 %collective-permute-start.9 = (bf16[4,128,2048]{2,1,0:T(8,128)(2,1)}, bf16[4,128,2048]{2,1,0:T(8,128)(2,1)}, u32[]{:S(2)}, u32[]{:S(2)}) collective-permute-start(bf16[4,128,2048]{2,1,0:T(8,128)(2,1)} %refs_2_.1), channel_id=1, source_target_pairs={{0,20},{8,24},{16,0},{24,12},{4,16},{12,28},{20,4},{28,8},{1,21},{... | collective-permute-start | bytes 6291464 | tf_op jit(solution)/shard_map/ppermute | solution.py:195
  2.1 67.1 %collective-permute-start = (bf16[4,128,2048]{2,1,0:T(8,128)(2,1)}, bf16[4,128,2048]{2,1,0:T(8,128)(2,1)}, u32[]{:S(2)}, u32[]{:S(2)}) collective-permute-start(bf16[4,128,2048]{2,1,0:T(8,128)(2,1)} %refs_2_.1), channel_id=1, source_target_pairs={{0,8},{8,0},{1,9},{9,1},{2,10},{10,2},{3,11},{11,3},{4,12},{12,4},... | collective-permute-start | bytes 6291464 | tf_op jit(solution)/shard_map/ppermute | solution.py:194
  27.3 50.6 %collective-permute-start.10 = (bf16[4,128,2048]{2,1,0:T(8,128)(2,1)}, bf16[4,128,2048]{2,1,0:T(8,128)(2,1)}, u32[]{:S(2)}, u32[]{:S(2)}) collective-permute-start(bf16[4,128,2048]{2,1,0:T(8,128)(2,1)} %collective-permute-done.9.refs_2_), channel_id=1, source_target_pairs={{0,8},{8,0},{1,9},{9,1},{2,10},{10,2},{3,11},{11,3},{4,12},{12,4},... | collective-permute-start | bytes 6291464 | tf_op jit(solution)/shard_map/ppermute | solution.py:200
  30.6 10.1 %collective-permute-start.4 = (bf16[64,2048]{1,0:T(8,128)(2,1)S(1)}, bf16[64,2048]{1,0:T(8,128)(2,1)S(1)}, u32[]{:S(2)}, u32[]{:S(2)}) collective-permute-start(bf16[64,2048]{1,0:T(8,128)(2,1)S(1)} %get-tuple-element.23), channel_id=1, source_target_pairs={{0,224},{32,0},{64,32},{96,64},{128,96},{160,128},{192,160},{224,1... | collective-permute-start | bytes 786440 | tf_op jit(solution)/shard_map/ppermute | solution.py:187
  35.1 8.8 %collective-permute-start.2 = (bf16[64,2048]{1,0:T(8,128)(2,1)S(1)}, bf16[64,2048]{1,0:T(8,128)(2,1)S(1)}, u32[]{:S(2)}, u32[]{:S(2)}) collective-permute-start(bf16[64,2048]{1,0:T(8,128)(2,1)S(1)} %get-tuple-element.23), channel_id=1, source_target_pairs={{0,32},{32,64},{64,96},{96,128},{128,160},{160,192},{192,224},{224... | collective-permute-start | bytes 786440 | tf_op jit(solution)/shard_map/ppermute | solution.py:186
  35.1 11.3 %collective-permute-start.3 = (bf16[64,2048]{1,0:T(8,128)(2,1)S(1)}, bf16[64,2048]{1,0:T(8,128)(2,1)S(1)}, u32[]{:S(2)}, u32[]{:S(2)}) collective-permute-start(bf16[64,2048]{1,0:T(8,128)(2,1)S(1)} %get-tuple-element.24), channel_id=1, source_target_pairs={{0,224},{32,0},{64,32},{96,64},{128,96},{160,128},{192,160},{224,1... | collective-permute-start | bytes 786440 | tf_op jit(solution)/shard_map/ppermute | solution.py:187
  40.8 8.8 %collective-permute-start.1 = (bf16[64,2048]{1,0:T(8,128)(2,1)S(1)}, bf16[64,2048]{1,0:T(8,128)(2,1)S(1)}, u32[]{:S(2)}, u32[]{:S(2)}) collective-permute-start(bf16[64,2048]{1,0:T(8,128)(2,1)S(1)} %get-tuple-element.24), channel_id=1, source_target_pairs={{0,32},{32,64},{64,96},{96,128},{128,160},{160,192},{192,224},{224... | collective-permute-start | bytes 786440 | tf_op jit(solution)/shard_map/ppermute | solution.py:186
  43.9 8.1 %collective-permute-start.8 = (bf16[64,2048]{1,0:T(8,128)(2,1)S(1)}, bf16[64,2048]{1,0:T(8,128)(2,1)S(1)}, u32[]{:S(2)}, u32[]{:S(2)}) collective-permute-start(bf16[64,2048]{1,0:T(8,128)(2,1)S(1)} %collective-permute-done.4.refs_7_), channel_id=1, source_target_pairs={{0,224},{32,0},{64,32},{96,64},{128,96},{160,128},{192,160},{224,1... | collective-permute-start | bytes 786440 | tf_op jit(solution)/shard_map/ppermute | solution.py:187
  46.4 9.0 %collective-permute-start.6 = (bf16[64,2048]{1,0:T(8,128)(2,1)S(1)}, bf16[64,2048]{1,0:T(8,128)(2,1)S(1)}, u32[]{:S(2)}, u32[]{:S(2)}) collective-permute-start(bf16[64,2048]{1,0:T(8,128)(2,1)S(1)} %collective-permute-done.2.refs_5_), channel_id=1, source_target_pairs={{0,32},{32,64},{64,96},{96,128},{128,160},{160,192},{192,224},{224... | collective-permute-start | bytes 786440 | tf_op jit(solution)/shard_map/ppermute | solution.py:186
  49.5 11.2 %collective-permute-start.5 = (bf16[64,2048]{1,0:T(8,128)(2,1)S(1)}, bf16[64,2048]{1,0:T(8,128)(2,1)S(1)}, u32[]{:S(2)}, u32[]{:S(2)}) collective-permute-start(bf16[64,2048]{1,0:T(8,128)(2,1)S(1)} %collective-permute-done.1.refs_4_), channel_id=1, source_target_pairs={{0,32},{32,64},{64,96},{96,128},{128,160},{160,192},{192,224},{224... | collective-permute-start | bytes 786440 | tf_op jit(solution)/shard_map/ppermute | solution.py:186
  52.0 9.5 %collective-permute-start.7 = (bf16[64,2048]{1,0:T(8,128)(2,1)S(1)}, bf16[64,2048]{1,0:T(8,128)(2,1)S(1)}, u32[]{:S(2)}, u32[]{:S(2)}) collective-permute-start(bf16[64,2048]{1,0:T(8,128)(2,1)S(1)} %collective-permute-done.3.refs_6_), channel_id=1, source_target_pairs={{0,224},{32,0},{64,32},{96,64},{128,96},{160,128},{192,160},{224,1... | collective-permute-start | bytes 786440 | tf_op jit(solution)/shard_map/ppermute | solution.py:187
  55.4 10.4 %collective-permute-start.14 = (bf16[64,2048]{1,0:T(8,128)(2,1)S(1)}, bf16[64,2048]{1,0:T(8,128)(2,1)S(1)}, u32[]{:S(2)}, u32[]{:S(2)}) collective-permute-start(bf16[64,2048]{1,0:T(8,128)(2,1)S(1)} %collective-permute-done.8.refs_6_.refs_11_), channel_id=1, source_target_pairs={{0,224},{32,0},{64,32},{96,64},{128,96},{160,128},{192,160},{224,1... | collective-permute-start | bytes 786440 | tf_op jit(solution)/shard_map/ppermute | solution.py:187
  60.8 8.5 %collective-permute-start.11 = (bf16[64,2048]{1,0:T(8,128)(2,1)S(1)}, bf16[64,2048]{1,0:T(8,128)(2,1)S(1)}, u32[]{:S(2)}, u32[]{:S(2)}) collective-permute-start(bf16[64,2048]{1,0:T(8,128)(2,1)S(1)} %collective-permute-done.5.refs_3_.refs_8_), channel_id=1, source_target_pairs={{0,32},{32,64},{64,96},{96,128},{128,160},{160,192},{192,224},{224... | collective-permute-start | bytes 786440 | tf_op jit(solution)/shard_map/ppermute | solution.py:186
  60.8 0.7 copy-start.1
  61.5 21.7 %collective-permute-start.12 = (bf16[64,2048]{1,0:T(8,128)(2,1)S(1)}, bf16[64,2048]{1,0:T(8,128)(2,1)S(1)}, u32[]{:S(2)}, u32[]{:S(2)}) collective-permute-start(bf16[64,2048]{1,0:T(8,128)(2,1)S(1)} %collective-permute-done.6.refs_4_.refs_9_), channel_id=1, source_target_pairs={{0,32},{32,64},{64,96},{96,128},{128,160},{160,192},{192,224},{224... | collective-permute-start | bytes 786440 | tf_op jit(solution)/shard_map/ppermute | solution.py:186
  65.8 17.4 %collective-permute-start.13 = (bf16[64,2048]{1,0:T(8,128)(2,1)S(1)}, bf16[64,2048]{1,0:T(8,128)(2,1)S(1)}, u32[]{:S(2)}, u32[]{:S(2)}) collective-permute-start(bf16[64,2048]{1,0:T(8,128)(2,1)S(1)} %collective-permute-done.7.refs_5_.refs_10_), channel_id=1, source_target_pairs={{0,224},{32,0},{64,32},{96,64},{128,96},{160,128},{192,160},{224,1... | collective-permute-start | bytes 786440 | tf_op jit(solution)/shard_map/ppermute | solution.py:187
  69.2 17.6 %collective-permute-start.16 = (bf16[64,2048]{1,0:T(8,128)(2,1)S(1)}, bf16[64,2048]{1,0:T(8,128)(2,1)S(1)}, u32[]{:S(2)}, u32[]{:S(2)}) collective-permute-start(bf16[64,2048]{1,0:T(8,128)(2,1)S(1)} %collective-permute-done.14.refs_7_), channel_id=1, source_target_pairs={{0,224},{32,0},{64,32},{96,64},{128,96},{160,128},{192,160},{224,1... | collective-permute-start | bytes 786440 | tf_op jit(solution)/shard_map/ppermute | solution.py:208
  69.3 17.6 %collective-permute-start.15 = (bf16[64,2048]{1,0:T(8,128)(2,1)S(1)}, bf16[64,2048]{1,0:T(8,128)(2,1)S(1)}, u32[]{:S(2)}, u32[]{:S(2)}) collective-permute-start(bf16[64,2048]{1,0:T(8,128)(2,1)S(1)} %collective-permute-done.11.refs_4_), channel_id=1, source_target_pairs={{0,32},{32,64},{64,96},{96,128},{128,160},{160,192},{192,224},{224... | collective-permute-start | bytes 786440 | tf_op jit(solution)/shard_map/ppermute | solution.py:206
  83.3 3.6 %copy-start = (bf16[128,2048]{1,0:T(8,128)(2,1)S(1)}, bf16[128,2048]{1,0:T(8,128)(2,1)}, u32[]{:S(2)}) copy-start(bf16[128,2048]{1,0:T(8,128)(2,1)} %refs_4_.1) | copy-start | bytes 1572868
  86.8 16.6 %copy-start.2 = (s32[4,4]{1,0:T(4,128)S(1)}, s32[4,4]{1,0:T(4,128)}, u32[]{:S(2)}) copy-start(s32[4,4]{1,0:T(4,128)} %param.6) | copy-start | bytes 196
  91.5 18.9 %all-to-all-start = ((f32[32,1,128]{2,1,0:T(1,128)}), f32[32,1,128]{2,1,0:T(1,128)S(1)}, u32[]{:S(2)}, u32[]{:S(2)}) async-start(f32[32,1,128]{2,1,0:T(1,128)} %bitcast.4), calls=%async_computation | async-start | bytes 32768 | tf_op jit(solution)/shard_map/all_to_all | solution.py:226
where the time goes:
time: 125 us; the launch traced here: 124 us
  waiting for transfers between devices  52.1 us (42%)
  starting transfers between devices  35.5 us (28%)
  Pallas kernels  19.6 us (16%)
  blocking collectives  12.9 us (10%)
  local copies, waits for them, and re-layouts  2.91 us (2%)
  other arithmetic  1.25 us (1%)
    ppermute x1, waiting for transfers between devices, per_device(): across = lax.ppermute(hidden, ('yl', 'c', 'yh'), across_y())  22.8 us
    pallas_call x5, Pallas kernels, score_blocks(): pl.pallas_call(functools.partial(scores_kernel, list(fresh), list(stores)...  19.5 us
    ppermute x6, starting transfers between devices, forward(): down[k] = lax.ppermute(down[k], 'z', around(8, -1))  15.2 us
    all_to_all x1, blocking collectives, per_device(): lax.all_to_all(copies, ('z', 'yl', 'c'), split_axis=0, concat_axis=0, til...  12.9 us
    all_to_all x1, starting transfers between devices, per_device(): lax.all_to_all(message, ('yl', 'c', 'yh', 'x'), split_axis=0, concat_axis...  12 us
    ppermute x6, waiting for transfers between devices, forward(): down[k] = lax.ppermute(down[k], 'z', around(8, -1))  11.9 us
    ppermute x6, waiting for transfers between devices, forward(): up[k] = lax.ppermute(up[k], 'z', around(8, 1))  10.7 us
    all_to_all x1, waiting for transfers between devices, per_device(): lax.all_to_all(message, ('yl', 'c', 'yh', 'x'), split_axis=0, concat_axis...  6.75 us
  transfers between devices with their start and end apart: 18, of which 9 were waited for; matrix products, arithmetic and copies ran while one was open for 1% of the time, Pallas kernels for 13%

commit v1 on v0

--- a/solution.py
+++ b/solution.py
@@ -25,44 +25,55 @@
     return [(place(y, core), place((y + 2 * core - 1) % 4, core)) for y in range(4) for core in (0, 1)]
 
 
-def scores_kernel(fresh_counts, held, blocks, places, *refs):
+def scores_kernel(done_near, before_count, fresh_counts, held, blocks, places, *refs):
     refs = list(refs)
     first_ref, wanted_ref = refs.pop(0), refs.pop(0)
-    stores = {b: refs.pop(0) for b in held}
+    before = [refs.pop(0) for _ in range(before_count)]
+    place_of = {}
+    for group in held:
+        ref = refs.pop(0)
+        place_of |= {b: ref.at[n] if len(ref.shape) == 4 else ref for n, b in enumerate(group)}
     fresh_refs = {b: refs.pop(0) for b in fresh_counts}
     head_refs = [refs.pop(0) for _ in places]
     out = refs.pop(0)
     copies = {}
     if fresh_counts:
-        stores[min(fresh_counts)], sems = refs
+        kept, sems = refs
+        place_of |= {b: kept.at[n] for n, b in enumerate(fresh_counts)}
         for b, ref in fresh_refs.items():
             for half in range(2):
                 tokens = pl.ds(64 * half, 64)
                 copies[b, half] = pltpu.make_async_copy(
                     ref.at[:, tokens],
-                    stores[b - b % 2].at[b % 2, :, tokens],
+                    place_of[b].at[:, tokens],
                     sems.at[len(copies)],
                 )
         queue = list(copies.values())
         for copy in queue[:2]:
             copy.start()
         queue = queue[2:]
-    groups, sizes = [[]], [0]
-    for place, ref in zip(places, head_refs):
-        if sizes[-1] + ref.shape[0] > 256:
-            groups.append([])
-            sizes.append(0)
-        groups[-1].append((place, ref))
-        sizes[-1] += ref.shape[0]
+
+    def grouped(b):
+        groups, size = [[]], 0
+        for place, ref in zip(places, head_refs):
+            if b < 2 and place in done_near:
+                continue
+            if size + ref.shape[0] > 256:
+                groups.append([])
+                size = 0
+            groups[-1].append((place, ref))
+            size += ref.shape[0]
+        return groups
+
     for n, b in enumerate(blocks):
         for half in range(2):
-            if copies:
+            if (b, half) in copies:
                 copies[b, half].wait()
                 if queue:
                     queue.pop(0).start()
             rows = jnp.concatenate(
                 [
-                    stores[b - b % 2][b % 2, k, 16 * v : 16 * v + 16, :]
+                    place_of[b][k, 16 * v : 16 * v + 16, :]
                     for v in range(4 * half, 4 * half + 4)
                     for k in range(4)
                 ],
@@ -71,7 +82,7 @@
             lanes = slice(256 * half, 256 * half + 256)
             wanted = wanted_ref[0:1, lanes]
             pieces = []
-            for group in groups:
+            for group in grouped(b):
                 head = jnp.concatenate([ref[...] for _, ref in group], axis=0)
                 logits = lax.dot_general(
                     head, rows, (((1,), (1,)), ((), ())), preferred_element_type=jnp.float32
@@ -92,29 +103,47 @@
             summed = sum(
                 jnp.sum(jnp.exp(part - highest), axis=0, keepdims=True) for part in others
             )
-            out[n, 0:1, lanes] = highest
-            out[n, 1:2, lanes] = summed
-            out[n, 2:3, lanes] = target_logit
-
-
-def score_blocks(stores, fresh, blocks, pieces, first, wanted):
+            if not before:
+                out[n, 0:1, lanes] = highest
+                out[n, 1:2, lanes] = summed
+                out[n, 2:3, lanes] = target_logit
+                continue
+            for ref in before:
+                earlier, raised = ref[n, 0:1, lanes], jnp.maximum(highest, ref[n, 0:1, lanes])
+                summed = summed * jnp.exp(highest - raised) + ref[n, 1:2, lanes] * jnp.exp(
+                    earlier - raised
+                )
+                highest = raised
+                target_logit = target_logit + ref[n, 2:3, lanes]
+            total, message = highest + jnp.log(summed), []
+            left = lax.broadcasted_iota(jnp.int32, (1, 128), 1) < 64
+            for k in range(2):
+                part, hit = total[:, 128 * k : 128 * k + 128], target_logit[:, 128 * k : 128 * k + 128]
+                message.append(jnp.where(left, part, pltpu.roll(hit, 64, 1)))
+                message.append(jnp.where(left, pltpu.roll(part, 64, 1), hit))
+            owner = first_ref[first_ref.shape[0] - 1] ^ b
+            out[owner, 4 * half : 4 * half + 4, :] = jnp.concatenate(message, axis=0)
+
+
+def score_blocks(stores, fresh, blocks, pieces, first, wanted, before=(), done_near=()):
     heads = [head for head, _ in pieces]
     vmem = pl.BlockSpec(memory_space=pltpu.VMEM)
     head_rows = sum(head.shape[0] for head in heads)
-    outs = [jax.ShapeDtypeStruct((len(blocks), 3, 512), jnp.float32)]
+    shape = (4, 8, 128) if before else (len(blocks), 3, 512)
+    outs = [jax.ShapeDtypeStruct(shape, jnp.float32)]
     if fresh:
-        outs.append(jax.ShapeDtypeStruct((2, 4, 128, 2048), jnp.bfloat16))
+        outs.append(jax.ShapeDtypeStruct((len(fresh), 4, 128, 2048), jnp.bfloat16))
     results = pl.pallas_call(
         functools.partial(
-            scores_kernel, list(fresh), list(stores), blocks, [place for _, place in pieces]
+            scores_kernel, done_near, len(before), list(fresh), list(stores), blocks, [place for _, place in pieces]
         ),
         in_specs=[pl.BlockSpec(memory_space=pltpu.SMEM), vmem]
-        + [vmem] * len(stores)
+        + [vmem] * (len(before) + len(stores))
         + [pl.BlockSpec(memory_space=pltpu.HBM)] * len(fresh)
         + [vmem] * len(heads),
         out_specs=[vmem] * len(outs),
         out_shape=outs,
-        scratch_shapes=[pltpu.SemaphoreType.DMA((4,))] if fresh else [],
+        scratch_shapes=[pltpu.SemaphoreType.DMA((2 * len(fresh),))] if fresh else [],
         compiler_params=pltpu.CompilerParams(vmem_limit_bytes=12 << 20),
         cost_estimate=pl.CostEstimate(
             flops=2 * 512 * len(blocks) * head_rows * 2048,
@@ -124,6 +153,7 @@
     )(
         first,
         wanted,
+        *before,
         *stores.values(),
         *[pltpu.with_memory_space_constraint(rows, pltpu.HBM) for rows in fresh.values()],
         *heads,
@@ -172,33 +202,37 @@
     vocab_index = lax.axis_index(("yh", "x"))
     part_rows = head_rows // PARTS
 
-    place = jnp.arange(8 * PARTS, dtype=jnp.int32)
+    place = jnp.arange(8 * PARTS + 1, dtype=jnp.int32)
     source = (((z - place // PARTS) & 7) * 4 + yl * 2 + core) * 8 + vocab_index
     first = source * head_rows + place % PARTS * part_rows
+    first = jnp.where(jnp.arange(8 * PARTS + 1) < 8 * PARTS, first, yl * 2 + core)
 
     swap = [(0, 1), (1, 0)]
-    up = [unembedding[k * part_rows : (k + 1) * part_rows] for k in range(PARTS)]
-    down = list(up)
-    gathered = [[(unembedding, 0)]]
+    up, down, gathered = [unembedding], [unembedding], [[(unembedding, 0)]]
 
     def forward(step):
-        for k in range(PARTS):
+        for k in range(len(up)):
             up[k] = lax.ppermute(up[k], "z", around(8, 1))
             down[k] = lax.ppermute(down[k], "z", around(8, -1))
         gathered.append(
-            [(up[k], PARTS * step + k) for k in range(PARTS)]
-            + [(down[k], PARTS * (8 - step) + k) for k in range(PARTS)]
+            [(rows, PARTS * step + k) for k, rows in enumerate(up)]
+            + [(rows, PARTS * (8 - step) + k) for k, rows in enumerate(down)]
         )
 
     forward(1)
     beside = lax.ppermute(hidden, "c", swap)
     across = lax.ppermute(hidden, ("yl", "c", "yh"), across_y())
     wanted = wanted_rows(targets)
+    near_found, near = score_blocks({(1,): beside}, {0: hidden}, [1, 0], gathered[0], first, wanted)
+    up = [up[0][k * part_rows : (k + 1) * part_rows] for k in range(PARTS)]
+    down = [down[0][k * part_rows : (k + 1) * part_rows] for k in range(PARTS)]
     forward(2)
-    near_found, near = score_blocks({}, {0: hidden, 1: beside}, [0, 1], gathered[1], first, wanted)
+    held = {(0,): near, (1,): beside}
+    (latter,) = score_blocks(held, {}, [0, 1], gathered[1], first, wanted)
+    near_found = combine(near_found[::-1], latter)
     forward(3)
     diagonal = lax.ppermute(across, "c", swap)
-    (latter,) = score_blocks({0: near}, {}, [0, 1], gathered[2], first, wanted)
+    (latter,) = score_blocks(held, {}, [0, 1], gathered[2], first, wanted)
     near_found = combine(near_found, latter)
     last = []
     for k in range(PARTS):
@@ -206,23 +240,17 @@
             last.append((lax.ppermute(up[k], "z", around(8, 1)), PARTS * 4 + k))
         else:
             last.append((lax.ppermute(down[k], "z", around(8, -1)), PARTS * 4 + k))
+    early = gathered[1] + gathered[2]
     (wanted_far,) = after((wanted,), (near_found,))
-    far_found, far = score_blocks(
-        {}, {2: across, 3: diagonal}, [2, 3], gathered[1] + gathered[2], first, wanted_far
-    )
-    found = jnp.concatenate([near_found, far_found])
-    stores, every = {0: near, 2: far}, [0, 1, 2, 3]
+    far_found, far = score_blocks({(3,): diagonal}, {2: across}, [3, 2], early, first, wanted_far)
+    found = jnp.concatenate([near_found, far_found[::-1]])
+    stores, every = held | {(2,): far, (3,): diagonal}, [0, 1, 2, 3]
     (latter,) = score_blocks(stores, {}, every, gathered[3], first, wanted_far)
-    found = combine(found, latter)
-    (wanted_last,) = after((wanted,), (found,))
-    (latter,) = score_blocks(stores, {}, every, gathered[0] + last, first, wanted_last)
-    found = combine(found, latter)
-
-    both = jnp.stack([found[:, 0] + jnp.log(found[:, 1]), found[:, 2]], axis=1)
-    both = both.reshape(2, 2, 2, 8, 64)
-    both = jnp.where(yl == 1, both[::-1], both)
-    both = jnp.where(core == 1, both[:, ::-1], both)
-    message = both.transpose(0, 1, 3, 2, 4).reshape(32, 1, 128)
+    (wanted_last,) = after((wanted,), (latter,))
+    (message,) = score_blocks(
+        stores, {}, every, gathered[0] + last, first, wanted_last, (found, latter), (0,)
+    )
+    message = message.reshape(32, 1, 128)
     received = lax.all_to_all(
         message, ("yl", "c", "yh", "x"), split_axis=0, concat_axis=0, tiled=True
     ).reshape(32, 128)

time: 125 us -> 121 us (0.968)
  waiting for transfers between devices: 52.1 us -> 40.2 us
  Pallas kernels: 19.6 us -> 24.2 us
  local copies, waits for them, and re-layouts: 2.91 us -> 6.7 us
    ppermute x6 -> x5, waiting for transfers between devices: 11.9 us -> 0.01 us  [forward(): down[k] = lax.ppermute(down[k], 'z', around(8, -1))]
    ppermute x1, waiting for transfers between devices: 22.8 us -> 17.2 us  [per_device(): across = lax.ppermute(hidden, ('yl', 'c', 'yh'), across_y())]
    ppermute x6 -> x5, waiting for transfers between devices: 10.7 us -> 16.2 us  [forward(): up[k] = lax.ppermute(up[k], 'z', around(8, 1))]
    unnamed x6 -> x16, local copies, waits for them, and re-layouts: 0.67 us -> 5.56 us
    ppermute x6 -> x5, starting transfers between devices: 15.2 us -> 10.3 us  [forward(): down[k] = lax.ppermute(down[k], 'z', around(8, -1))]
    pallas_call x5 -> x6, Pallas kernels: 19.5 us -> 24.2 us  [score_blocks(): pl.pallas_call(functools.partial(scores_kernel, done_near, len(before), l...]
    ppermute x6 -> x5, starting transfers between devices: 0.1 us -> 3.9 us  [forward(): up[k] = lax.ppermute(up[k], 'z', around(8, 1))]
  transfers between devices with their start and end apart: 18 -> 16, of which waited for: 9 -> 5; matrix products, arithmetic and copies ran while one was open for 1% -> 1% of each run, Pallas kernels for 13% -> 16%
where the time goes in v1:
time: 121 us
  waiting for transfers between devices  40.2 us (33%)
  starting transfers between devices  34.8 us (29%)
  Pallas kernels  24.2 us (20%)
  blocking collectives  13.6 us (11%)
  local copies, waits for them, and re-layouts  6.7 us (6%)
    pallas_call x6, Pallas kernels, score_blocks(): pl.pallas_call(functools.partial(scores_kernel, done_near, len(before), l...  24.2 us
    ppermute x1, waiting for transfers between devices, per_device(): across = lax.ppermute(hidden, ('yl', 'c', 'yh'), across_y())  17.2 us
    ppermute x5, waiting for transfers between devices, forward(): up[k] = lax.ppermute(up[k], 'z', around(8, 1))  16.2 us
    all_to_all x1, blocking collectives, per_device(): lax.all_to_all(copies, ('z', 'yl', 'c'), split_axis=0, concat_axis=0, til...  13.6 us
    all_to_all x1, starting transfers between devices, per_device(): lax.all_to_all(message, ('yl', 'c', 'yh', 'x'), split_axis=0, concat_axis...  11.1 us
    ppermute x5, starting transfers between devices, forward(): down[k] = lax.ppermute(down[k], 'z', around(8, -1))  10.3 us
    all_to_all x1, waiting for transfers between devices, per_device(): lax.all_to_all(message, ('yl', 'c', 'yh', 'x'), split_axis=0, concat_axis...  6.76 us
    unnamed x16, local copies, waits for them, and re-layouts  5.56 us
  transfers between devices with their start and end apart: 16, of which 5 were waited for; matrix products, arithmetic and copies ran while one was open for 1% of the time, Pallas kernels for 16%

profile of v1, /device:TPU:1, one launch (start us, length us, event | category | flops | bytes accessed | tf_op | source)
XLA Modules:
  0.0 120.8 jit_solution(6611615916870698079)
XLA Ops:
  0.0 2.1 %collective-permute-start.7 = (bf16[4,128,2048]{2,1,0:T(8,128)(2,1)}, bf16[4,128,2048]{2,1,0:T(8,128)(2,1)}, u32[]{:S(2)}, u32[]{:S(2)}) collective-permute-start(bf16[4,128,2048]{2,1,0:T(8,128)(2,1)} %refs_3_.1), channel_id=1, source_target_pairs={{0,20},{8,24},{16,0},{24,12},{4,16},{12,28},{20,4},{28,8},{1,21},{... | collective-permute-start | bytes 6291464 | tf_op jit(solution)/shard_map/ppermute | solution.py:224
  2.1 2.4 %collective-permute-start = (bf16[4,128,2048]{2,1,0:T(8,128)(2,1)}, bf16[4,128,2048]{2,1,0:T(8,128)(2,1)S(1)}, u32[]{:S(2)}, u32[]{:S(2)}) collective-permute-start(bf16[4,128,2048]{2,1,0:T(8,128)(2,1)} %refs_3_.1), channel_id=1, source_target_pairs={{0,8},{8,0},{1,9},{9,1},{2,10},{10,2},{3,11},{11,3},{4,12},{12,4},... | collective-permute-start | bytes 6291464 | tf_op jit(solution)/shard_map/ppermute | solution.py:223
  4.5 1.6 %collective-permute-start.1 = (bf16[128,2048]{1,0:T(8,128)(2,1)}, bf16[128,2048]{1,0:T(8,128)(2,1)S(1)}, u32[]{:S(2)}, u32[]{:S(2)}) collective-permute-start(bf16[128,2048]{1,0:T(8,128)(2,1)} %refs_8_.1), channel_id=1, source_target_pairs={{0,32},{32,64},{64,96},{96,128},{128,160},{160,192},{192,224},{224... | collective-permute-start | bytes 1572872 | tf_op jit(solution)/shard_map/ppermute | solution.py:215
  6.1 3.9 %collective-permute-start.2 = (bf16[128,2048]{1,0:T(8,128)(2,1)}, bf16[128,2048]{1,0:T(8,128)(2,1)S(1)}, u32[]{:S(2)}, u32[]{:S(2)}) collective-permute-start(bf16[128,2048]{1,0:T(8,128)(2,1)} %refs_8_.1), channel_id=1, source_target_pairs={{0,224},{32,0},{64,32},{96,64},{128,96},{160,128},{192,160},{224,1... | collective-permute-start | bytes 1572872 | tf_op jit(solution)/shard_map/ppermute | solution.py:216
  10.1 17.2 %collective-permute-done.7.refs_3_ = bf16[4,128,2048]{2,1,0:T(8,128)(2,1)} collective-permute-done((bf16[4,128,2048]{2,1,0:T(8,128)(2,1)}, bf16[4,128,2048]{2,1,0:T(8,128)(2,1)}, u32[]{:S(2)}, u32[]{:S(2)}) %collective-permute-start.7) | collective-permute-done | bytes 2097184 | tf_op jit(solution)/shard_map/ppermute | solution.py:224
  27.3 2.3 %collective-permute-start.8 = (bf16[4,128,2048]{2,1,0:T(8,128)(2,1)}, bf16[4,128,2048]{2,1,0:T(8,128)(2,1)}, u32[]{:S(2)}, u32[]{:S(2)}) collective-permute-start(bf16[4,128,2048]{2,1,0:T(8,128)(2,1)} %collective-permute-done.7.refs_3_), channel_id=1, source_target_pairs={{0,8},{8,0},{1,9},{9,1},{2,10},{10,2},{3,11},{11,3},{4,12},{12,4},... | collective-permute-start | bytes 6291464 | tf_op jit(solution)/shard_map/ppermute | solution.py:234
  29.6 0.0 collective-permute-done.1.refs_4_
  29.6 0.5 collective-permute-start.4
  30.1 1.6 %collective-permute-start.3 = (bf16[64,2048]{1,0:T(8,128)(2,1)S(1)}, bf16[64,2048]{1,0:T(8,128)(2,1)}, u32[]{:S(2)}, u32[]{:S(2)}) collective-permute-start(bf16[64,2048]{1,0:T(8,128)(2,1)S(1)} %get-tuple-element.26), channel_id=1, source_target_pairs={{0,32},{32,64},{64,96},{96,128},{128,160},{160,192},{192,224},{224... | collective-permute-start | bytes 786440 | tf_op jit(solution)/shard_map/ppermute | solution.py:215
  31.8 0.0 collective-permute-done.2.refs_5_
  31.8 0.8 fusion.16
  32.5 2.4 %collective-permute-start.6 = (bf16[64,2048]{1,0:T(8,128)(2,1)S(1)}, bf16[64,2048]{1,0:T(8,128)(2,1)}, u32[]{:S(2)}, u32[]{:S(2)}) collective-permute-start(bf16[64,2048]{1,0:T(8,128)(2,1)S(1)} %get-tuple-element.23), channel_id=1, source_target_pairs={{0,224},{32,0},{64,32},{96,64},{128,96},{160,128},{192,160},{224,1... | collective-permute-start | bytes 786440 | tf_op jit(solution)/shard_map/ppermute | solution.py:216
  35.0 5.8 %collective-permute-done.4.refs_5_.refs_7_ = bf16[64,2048]{1,0:T(8,128)(2,1)S(1)} collective-permute-done((bf16[64,2048]{1,0:T(8,128)(2,1)S(1)}, bf16[64,2048]{1,0:T(8,128)(2,1)S(1)}, u32[]{:S(2)}, u32[]{:S(2)}) %collective-permute-start.4) | collective-permute-done | bytes 262176 | tf_op jit(solution)/shard_map/ppermute | solution.py:215
  40.8 1.3 %collective-permute-start.5 = (bf16[64,2048]{1,0:T(8,128)(2,1)}, bf16[64,2048]{1,0:T(8,128)(2,1)}, u32[]{:S(2)}, u32[]{:S(2)}) collective-permute-start(bf16[64,2048]{1,0:T(8,128)(2,1)} %get-tuple-element.24), channel_id=1, source_target_pairs={{0,224},{32,0},{64,32},{96,64},{128,96},{160,128},{192,160},{224,1... | collective-permute-start | bytes 786440 | tf_op jit(solution)/shard_map/ppermute | solution.py:216
  42.1 4.4 %collective-permute-done.3.refs_4_.refs_6_ = bf16[64,2048]{1,0:T(8,128)(2,1)} collective-permute-done((bf16[64,2048]{1,0:T(8,128)(2,1)S(1)}, bf16[64,2048]{1,0:T(8,128)(2,1)}, u32[]{:S(2)}, u32[]{:S(2)}) %collective-permute-start.3) | collective-permute-done | bytes 262176 | tf_op jit(solution)/shard_map/ppermute | solution.py:215
  46.5 2.7 %collective-permute-start.12 = (bf16[64,2048]{1,0:T(8,128)(2,1)}, bf16[64,2048]{1,0:T(8,128)(2,1)}, u32[]{:S(2)}, u32[]{:S(2)}) collective-permute-start(bf16[64,2048]{1,0:T(8,128)(2,1)} %collective-permute-done.6.refs_7_.refs_9_), channel_id=1, source_target_pairs={{0,224},{32,0},{64,32},{96,64},{128,96},{160,128},{192,160},{224,1... | collective-permute-start | bytes 786440 | tf_op jit(solution)/shard_map/ppermute | solution.py:216
  49.2 0.1 shard_map.46.refs_1_
  49.3 0.0 collective-permute-done.5.refs_6_.refs_8_
  49.3 0.1 collective-permute-start.10
  49.4 5.9 %collective-permute-done.9.refs_6_ = bf16[64,2048]{1,0:T(8,128)(2,1)} collective-permute-done((bf16[64,2048]{1,0:T(8,128)(2,1)}, bf16[64,2048]{1,0:T(8,128)(2,1)}, u32[]{:S(2)}, u32[]{:S(2)}) %collective-permute-start.9) | collective-permute-done | bytes 262176 | tf_op jit(solution)/shard_map/ppermute | solution.py:215
  55.3 0.0 collective-permute-start.11
  55.3 0.0 collective-permute-done.12.refs_9_
  55.3 1.5 %collective-permute-start.13 = (bf16[64,2048]{1,0:T(8,128)(2,1)}, bf16[64,2048]{1,0:T(8,128)(2,1)}, u32[]{:S(2)}, u32[]{:S(2)}) collective-permute-start(bf16[64,2048]{1,0:T(8,128)(2,1)} %collective-permute-done.9.refs_6_), channel_id=1, source_target_pairs={{0,32},{32,64},{64,96},{96,128},{128,160},{160,192},{192,224},{224... | collective-permute-start | bytes 786440 | tf_op jit(solution)/shard_map/ppermute | solution.py:240
  56.8 1.2 %collective-permute-start.14 = (bf16[64,2048]{1,0:T(8,128)(2,1)}, bf16[64,2048]{1,0:T(8,128)(2,1)}, u32[]{:S(2)}, u32[]{:S(2)}) collective-permute-start(bf16[64,2048]{1,0:T(8,128)(2,1)} %collective-permute-done.12.refs_9_), channel_id=1, source_target_pairs={{0,224},{32,0},{64,32},{96,64},{128,96},{160,128},{192,160},{224,1... | collective-permute-start | bytes 786440 | tf_op jit(solution)/shard_map/ppermute | solution.py:242
  58.0 1.0 copy-done.4
  59.0 3.3 %shard_map.47 = (f32[2,3,512]{2,1,0:T(4,128)S(1)}, bf16[1,4,128,2048]{3,2,1,0:T(8,128)(2,1)S(1)}) custom-call(s32[17]{0:T(128)S(1)} %compare_select_fusion.refs_0_, s32[1,512]{1,0:T(1,128)S(1)} %shard_map.46.refs_1_, bf16[4,128,2048]{2,1,0:T(8,128)(2,1)S(1)} %collective-permute-done.refs_2_.refs_3_.refs_5_, bf16[4,128,2048]{2,1,0:T(8,128)(2,1)} %refs_3_.1, ...), custom_call_target="tpu_custom_call" | custom-call | flops 536870912 | bytes 4718592 | tf_op jit(solution)/shard_map/pallas_call | solution.py:136
  62.4 3.3 %shard_map.49 = f32[2,3,512]{2,1,0:T(4,128)S(1)} custom-call(s32[17]{0:T(128)S(1)} %compare_select_fusion.refs_0_, s32[1,512]{1,0:T(1,128)S(1)} %shard_map.46.refs_1_, bf16[1,4,128,2048]{3,2,1,0:T(8,128)(2,1)S(1)} %get-tuple-element.12.refs_2_.refs_4_, bf16[4,128,2048]{2,1,0:T(8,128)(2,1)S(1)} %collective-permute-done.refs_2_.refs_3_.refs_5_, ...), custom_call_target="tpu_custom_call" | custom-call | flops 1073741824 | bytes 5242880 | tf_op jit(solution)/shard_map/pallas_call | solution.py:136
  65.7 2.1 %shard_map.48 = f32[2,3,512]{2,1,0:T(4,128)S(1)} custom-call(s32[17]{0:T(128)S(1)} %compare_select_fusion.refs_0_, s32[1,512]{1,0:T(1,128)S(1)} %shard_map.46.refs_1_, bf16[1,4,128,2048]{3,2,1,0:T(8,128)(2,1)S(1)} %get-tuple-element.12.refs_2_.refs_4_, bf16[4,128,2048]{2,1,0:T(8,128)(2,1)S(1)} %collective-permute-done.refs_2_.refs_3_.refs_5_, ...), custom_call_target="tpu_custom_call" | custom-call | flops 1073741824 | bytes 5242880 | tf_op jit(solution)/shard_map/pallas_call | solution.py:136
  67.8 5.2 %shard_map.50 = (f32[2,3,512]{2,1,0:T(4,128)S(1)}, bf16[1,4,128,2048]{3,2,1,0:T(8,128)(2,1)S(1)}) custom-call(s32[17]{0:T(128)S(1)} %compare_select_fusion.refs_0_, s32[1,512]{1,0:T(1,128)S(1)} %shard_map.46.refs_1_, bf16[4,128,2048]{2,1,0:T(8,128)(2,1)} %collective-permute-done.8.refs_2_.refs_5_.refs_7_, ...), custom_call_target="tpu_custom_call" | custom-call | flops 2147483648 | bytes 6291456 | tf_op jit(solution)/shard_map/pallas_call | solution.py:136
  73.0 1.3 %copy-done.2 = bf16[1,4,128,2048]{3,2,1,0:T(8,128)(2,1)} copy-done((bf16[1,4,128,2048]{3,2,1,0:T(8,128)(2,1)}, bf16[1,4,128,2048]{3,2,1,0:T(8,128)(2,1)S(1)}, u32[]{:S(2)}) %copy-start.2) | copy-done | bytes 2097176
  74.4 0.0 collective-permute-done.10.refs_7_
  74.4 0.0 collective-permute-done.11.refs_8_
  74.4 1.6 %copy-done.1 = bf16[1,4,128,2048]{3,2,1,0:T(8,128)(2,1)S(1)} copy-done((bf16[1,4,128,2048]{3,2,1,0:T(8,128)(2,1)S(1)}, bf16[1,4,128,2048]{3,2,1,0:T(8,128)(2,1)}, u32[]{:S(2)}) %copy-start.1) | copy-done | bytes 2097176
  76.0 1.6 %copy-done.3 = bf16[1,4,128,2048]{3,2,1,0:T(8,128)(2,1)S(1)} copy-done((bf16[1,4,128,2048]{3,2,1,0:T(8,128)(2,1)S(1)}, bf16[1,4,128,2048]{3,2,1,0:T(8,128)(2,1)}, u32[]{:S(2)}) %copy-start.3) | copy-done | bytes 2097176
  77.5 4.9 %shard_map.51.refs_3_ = f32[4,3,512]{2,1,0:T(4,128)S(1)} custom-call(s32[17]{0:T(128)S(1)} %compare_select_fusion.refs_0_, s32[1,512]{1,0:T(1,128)S(1)} %shard_map.46.refs_1_, bf16[1,4,128,2048]{3,2,1,0:T(8,128)(2,1)S(1)} %copy-done.1, bf16[4,128,2048]{2,1,0:T(8,128)(2,1)S(1)} %collective-permute-done.refs_2_.refs_3_.refs_5_, ...), custom_call_target="tpu_custom_call" | custom-call | flops 2147483648 | bytes 9437184 | tf_op jit(solution)/shard_map/pallas_call | solution.py:136
  82.5 0.0 copy-start.7
  82.5 5.4 %shard_map.52 = f32[4,8,128]{2,1,0:T(8,128)} custom-call(s32[17]{0:T(128)S(1)} %compare_select_fusion.refs_0_, s32[1,512]{1,0:T(1,128)S(1)} %shard_map.46.refs_1_, f32[4,3,512]{2,1,0:T(4,128)S(1)} %pad_maximum_fusion.refs_2_, f32[4,3,512]{2,1,0:T(4,128)S(1)} %shard_map.51.refs_3_, bf16[1,4,128,2048]{3,2,1,0:T(8,128)(2,1)S(1)} %copy-done.1, ...), custom_call_target="tpu_custom_call" | custom-call | flops 2147483648 | bytes 9437184 | tf_op jit(solution)/shard_map/pallas_call | solution.py:136
  87.9 11.1 %all-to-all-start = ((f32[32,1,128]{2,1,0:T(1,128)}), f32[32,1,128]{2,1,0:T(1,128)S(1)}, u32[]{:S(2)}, u32[]{:S(2)}) async-start(f32[32,1,128]{2,1,0:T(1,128)} %bitcast.2), calls=%async_computation | async-start | bytes 32768 | tf_op jit(solution)/shard_map/all_to_all | solution.py:254
  99.1 0.1 broadcast_in_dim.14
  99.2 0.1 reshape.25
  99.2 6.8 %all-to-all-done = f32[32,1,128]{2,1,0:T(1,128)S(1)} async-done(((f32[32,1,128]{2,1,0:T(1,128)}), f32[32,1,128]{2,1,0:T(1,128)S(1)}, u32[]{:S(2)}, u32[]{:S(2)}) %all-to-all-start) | async-done | bytes 16416 | tf_op jit(solution)/shard_map/all_to_all | solution.py:254
  106.0 0.1 exponential_reduce_fusion
  106.1 0.1 sub.85
  106.2 0.1 fusion.4
  106.3 0.1 pad_maximum_fusion.1
  106.4 13.6 %all_to_all.10 = f32[32,1,32]{2,1,0:T(1,128)S(1)} all-to-all(f32[32,1,32]{2,1,0:T(1,128)S(1)} %broadcast_in_dim.15), channel_id=1, replica_groups=mesh['z'=8,'yl'=2,'c'=2,'yh'=2,'x'=4] {'z','yl','c'}, dimensions={0} | all-to-all | bytes 8192 | tf_op jit(solution)/shard_map/all_to_all | solution.py:271
  120.0 0.1 fusion.19
  120.1 0.7 rsqrt_multiply_fusion
  (27 shorter events, 0.2 us)
Async XLA Ops:
  0.0 49.2 %copy-start.6 = (s32[128]{0:T(128)S(1)}, s32[128]{0:T(128)}, u32[]{:S(2)}) copy-start(s32[128]{0:T(128)} %param.5) | copy-start | bytes 1540
  0.0 27.3 %collective-permute-start.7 = (bf16[4,128,2048]{2,1,0:T(8,128)(2,1)}, bf16[4,128,2048]{2,1,0:T(8,128)(2,1)}, u32[]{:S(2)}, u32[]{:S(2)}) collective-permute-start(bf16[4,128,2048]{2,1,0:T(8,128)(2,1)} %refs_3_.1), channel_id=1, source_target_pairs={{0,20},{8,24},{16,0},{24,12},{4,16},{12,28},{20,4},{28,8},{1,21},{... | collective-permute-start | bytes 6291464 | tf_op jit(solution)/shard_map/ppermute | solution.py:224
  2.1 54.7 %collective-permute-start = (bf16[4,128,2048]{2,1,0:T(8,128)(2,1)}, bf16[4,128,2048]{2,1,0:T(8,128)(2,1)S(1)}, u32[]{:S(2)}, u32[]{:S(2)}) collective-permute-start(bf16[4,128,2048]{2,1,0:T(8,128)(2,1)} %refs_3_.1), channel_id=1, source_target_pairs={{0,8},{8,0},{1,9},{9,1},{2,10},{10,2},{3,11},{11,3},{4,12},{12,4},... | collective-permute-start | bytes 6291464 | tf_op jit(solution)/shard_map/ppermute | solution.py:223
  4.5 25.0 %collective-permute-start.1 = (bf16[128,2048]{1,0:T(8,128)(2,1)}, bf16[128,2048]{1,0:T(8,128)(2,1)S(1)}, u32[]{:S(2)}, u32[]{:S(2)}) collective-permute-start(bf16[128,2048]{1,0:T(8,128)(2,1)} %refs_8_.1), channel_id=1, source_target_pairs={{0,32},{32,64},{64,96},{96,128},{128,160},{160,192},{192,224},{224... | collective-permute-start | bytes 1572872 | tf_op jit(solution)/shard_map/ppermute | solution.py:215
  6.1 25.6 %collective-permute-start.2 = (bf16[128,2048]{1,0:T(8,128)(2,1)}, bf16[128,2048]{1,0:T(8,128)(2,1)S(1)}, u32[]{:S(2)}, u32[]{:S(2)}) collective-permute-start(bf16[128,2048]{1,0:T(8,128)(2,1)} %refs_8_.1), channel_id=1, source_target_pairs={{0,224},{32,0},{64,32},{96,64},{128,96},{160,128},{192,160},{224,1... | collective-permute-start | bytes 1572872 | tf_op jit(solution)/shard_map/ppermute | solution.py:216
  27.3 40.5 %collective-permute-start.8 = (bf16[4,128,2048]{2,1,0:T(8,128)(2,1)}, bf16[4,128,2048]{2,1,0:T(8,128)(2,1)}, u32[]{:S(2)}, u32[]{:S(2)}) collective-permute-start(bf16[4,128,2048]{2,1,0:T(8,128)(2,1)} %collective-permute-done.7.refs_3_), channel_id=1, source_target_pairs={{0,8},{8,0},{1,9},{9,1},{2,10},{10,2},{3,11},{11,3},{4,12},{12,4},... | collective-permute-start | bytes 6291464 | tf_op jit(solution)/shard_map/ppermute | solution.py:234
  29.6 11.2 %collective-permute-start.4 = (bf16[64,2048]{1,0:T(8,128)(2,1)S(1)}, bf16[64,2048]{1,0:T(8,128)(2,1)S(1)}, u32[]{:S(2)}, u32[]{:S(2)}) collective-permute-start(bf16[64,2048]{1,0:T(8,128)(2,1)S(1)} %get-tuple-element.25), channel_id=1, source_target_pairs={{0,32},{32,64},{64,96},{96,128},{128,160},{160,192},{192,224},{224... | collective-permute-start | bytes 786440 | tf_op jit(solution)/shard_map/ppermute | solution.py:215
  30.1 16.3 %collective-permute-start.3 = (bf16[64,2048]{1,0:T(8,128)(2,1)S(1)}, bf16[64,2048]{1,0:T(8,128)(2,1)}, u32[]{:S(2)}, u32[]{:S(2)}) collective-permute-start(bf16[64,2048]{1,0:T(8,128)(2,1)S(1)} %get-tuple-element.26), channel_id=1, source_target_pairs={{0,32},{32,64},{64,96},{96,128},{128,160},{160,192},{192,224},{224... | collective-permute-start | bytes 786440 | tf_op jit(solution)/shard_map/ppermute | solution.py:215
  32.5 13.9 %collective-permute-start.6 = (bf16[64,2048]{1,0:T(8,128)(2,1)S(1)}, bf16[64,2048]{1,0:T(8,128)(2,1)}, u32[]{:S(2)}, u32[]{:S(2)}) collective-permute-start(bf16[64,2048]{1,0:T(8,128)(2,1)S(1)} %get-tuple-element.23), channel_id=1, source_target_pairs={{0,224},{32,0},{64,32},{96,64},{128,96},{160,128},{192,160},{224,1... | collective-permute-start | bytes 786440 | tf_op jit(solution)/shard_map/ppermute | solution.py:216
  40.8 8.5 %collective-permute-start.5 = (bf16[64,2048]{1,0:T(8,128)(2,1)}, bf16[64,2048]{1,0:T(8,128)(2,1)}, u32[]{:S(2)}, u32[]{:S(2)}) collective-permute-start(bf16[64,2048]{1,0:T(8,128)(2,1)} %get-tuple-element.24), channel_id=1, source_target_pairs={{0,224},{32,0},{64,32},{96,64},{128,96},{160,128},{192,160},{224,1... | collective-permute-start | bytes 786440 | tf_op jit(solution)/shard_map/ppermute | solution.py:216
  46.5 8.8 %collective-permute-start.9 = (bf16[64,2048]{1,0:T(8,128)(2,1)}, bf16[64,2048]{1,0:T(8,128)(2,1)}, u32[]{:S(2)}, u32[]{:S(2)}) collective-permute-start(bf16[64,2048]{1,0:T(8,128)(2,1)} %collective-permute-done.3.refs_4_.refs_6_), channel_id=1, source_target_pairs={{0,32},{32,64},{64,96},{96,128},{128,160},{160,192},{192,224},{224... | collective-permute-start | bytes 786440 | tf_op jit(solution)/shard_map/ppermute | solution.py:215
  46.5 8.8 %collective-permute-start.12 = (bf16[64,2048]{1,0:T(8,128)(2,1)}, bf16[64,2048]{1,0:T(8,128)(2,1)}, u32[]{:S(2)}, u32[]{:S(2)}) collective-permute-start(bf16[64,2048]{1,0:T(8,128)(2,1)} %collective-permute-done.6.refs_7_.refs_9_), channel_id=1, source_target_pairs={{0,224},{32,0},{64,32},{96,64},{128,96},{160,128},{192,160},{224,1... | collective-permute-start | bytes 786440 | tf_op jit(solution)/shard_map/ppermute | solution.py:216
  49.3 25.1 %collective-permute-start.10 = (bf16[64,2048]{1,0:T(8,128)(2,1)S(1)}, bf16[64,2048]{1,0:T(8,128)(2,1)}, u32[]{:S(2)}, u32[]{:S(2)}) collective-permute-start(bf16[64,2048]{1,0:T(8,128)(2,1)S(1)} %collective-permute-done.4.refs_5_.refs_7_), channel_id=1, source_target_pairs={{0,32},{32,64},{64,96},{96,128},{128,160},{160,192},{192,224},{224... | collective-permute-start | bytes 786440 | tf_op jit(solution)/shard_map/ppermute | solution.py:215
  55.3 19.1 %collective-permute-start.11 = (bf16[64,2048]{1,0:T(8,128)(2,1)}, bf16[64,2048]{1,0:T(8,128)(2,1)}, u32[]{:S(2)}, u32[]{:S(2)}) collective-permute-start(bf16[64,2048]{1,0:T(8,128)(2,1)} %collective-permute-done.5.refs_6_.refs_8_), channel_id=1, source_target_pairs={{0,224},{32,0},{64,32},{96,64},{128,96},{160,128},{192,160},{224,1... | collective-permute-start | bytes 786440 | tf_op jit(solution)/shard_map/ppermute | solution.py:216
  55.3 27.2 %collective-permute-start.13 = (bf16[64,2048]{1,0:T(8,128)(2,1)}, bf16[64,2048]{1,0:T(8,128)(2,1)}, u32[]{:S(2)}, u32[]{:S(2)}) collective-permute-start(bf16[64,2048]{1,0:T(8,128)(2,1)} %collective-permute-done.9.refs_6_), channel_id=1, source_target_pairs={{0,32},{32,64},{64,96},{96,128},{128,160},{160,192},{192,224},{224... | collective-permute-start | bytes 786440 | tf_op jit(solution)/shard_map/ppermute | solution.py:240
  56.8 25.7 %collective-permute-start.14 = (bf16[64,2048]{1,0:T(8,128)(2,1)}, bf16[64,2048]{1,0:T(8,128)(2,1)}, u32[]{:S(2)}, u32[]{:S(2)}) collective-permute-start(bf16[64,2048]{1,0:T(8,128)(2,1)} %collective-permute-done.12.refs_9_), channel_id=1, source_target_pairs={{0,224},{32,0},{64,32},{96,64},{128,96},{160,128},{192,160},{224,1... | collective-permute-start | bytes 786440 | tf_op jit(solution)/shard_map/ppermute | solution.py:242
  58.0 1.0 copy-start.4
  62.4 3.3 %copy-start = (bf16[1,4,128,2048]{3,2,1,0:T(8,128)(2,1)}, bf16[1,4,128,2048]{3,2,1,0:T(8,128)(2,1)S(1)}, u32[]{:S(2)}) copy-start(bf16[1,4,128,2048]{3,2,1,0:T(8,128)(2,1)S(1)} %get-tuple-element.12.refs_2_.refs_4_) | copy-start | bytes 6291460
  73.0 1.3 %copy-start.2 = (bf16[1,4,128,2048]{3,2,1,0:T(8,128)(2,1)}, bf16[1,4,128,2048]{3,2,1,0:T(8,128)(2,1)S(1)}, u32[]{:S(2)}) copy-start(bf16[1,4,128,2048]{3,2,1,0:T(8,128)(2,1)S(1)} %get-tuple-element.14.refs_4_.refs_6_) | copy-start | bytes 6291460
  74.4 1.6 %copy-start.1 = (bf16[1,4,128,2048]{3,2,1,0:T(8,128)(2,1)S(1)}, bf16[1,4,128,2048]{3,2,1,0:T(8,128)(2,1)}, u32[]{:S(2)}) copy-start(bf16[1,4,128,2048]{3,2,1,0:T(8,128)(2,1)} %copy-done) | copy-start | bytes 6291460
  76.0 1.6 %copy-start.3 = (bf16[1,4,128,2048]{3,2,1,0:T(8,128)(2,1)S(1)}, bf16[1,4,128,2048]{3,2,1,0:T(8,128)(2,1)}, u32[]{:S(2)}) copy-start(bf16[1,4,128,2048]{3,2,1,0:T(8,128)(2,1)} %copy-done.2) | copy-start | bytes 6291460
  77.5 5.0 %copy-start.5 = (bf16[128,2048]{1,0:T(8,128)(2,1)S(1)}, bf16[128,2048]{1,0:T(8,128)(2,1)}, u32[]{:S(2)}) copy-start(bf16[128,2048]{1,0:T(8,128)(2,1)} %refs_8_.1) | copy-start | bytes 1572868
  82.5 16.6 %copy-start.7 = (s32[4,4]{1,0:T(4,128)S(1)}, s32[4,4]{1,0:T(4,128)}, u32[]{:S(2)}) copy-start(s32[4,4]{1,0:T(4,128)} %param.6) | copy-start | bytes 196
  87.9 18.1 %all-to-all-start = ((f32[32,1,128]{2,1,0:T(1,128)}), f32[32,1,128]{2,1,0:T(1,128)S(1)}, u32[]{:S(2)}, u32[]{:S(2)}) async-start(f32[32,1,128]{2,1,0:T(1,128)} %bitcast.2), calls=%async_computation | async-start | bytes 32768 | tf_op jit(solution)/shard_map/all_to_all | solution.py:254

commit v2 on v1

--- a/solution.py
+++ b/solution.py
@@ -65,7 +65,8 @@
             size += ref.shape[0]
         return groups
 
-    for n, b in enumerate(blocks):
+    for b in blocks:
+        n = sorted(blocks).index(b)
         for half in range(2):
             if (b, half) in copies:
                 copies[b, half].wait()
@@ -229,7 +230,7 @@
     forward(2)
     held = {(0,): near, (1,): beside}
     (latter,) = score_blocks(held, {}, [0, 1], gathered[1], first, wanted)
-    near_found = combine(near_found[::-1], latter)
+    near_found = combine(near_found, latter)
     forward(3)
     diagonal = lax.ppermute(across, "c", swap)
     (latter,) = score_blocks(held, {}, [0, 1], gathered[2], first, wanted)
@@ -243,7 +244,7 @@
     early = gathered[1] + gathered[2]
     (wanted_far,) = after((wanted,), (near_found,))
     far_found, far = score_blocks({(3,): diagonal}, {2: across}, [3, 2], early, first, wanted_far)
-    found = jnp.concatenate([near_found, far_found[::-1]])
+    found = jnp.concatenate([near_found, far_found])
     stores, every = held | {(2,): far, (3,): diagonal}, [0, 1, 2, 3]
     (latter,) = score_blocks(stores, {}, every, gathered[3], first, wanted_far)
     (wanted_last,) = after((wanted,), (latter,))

time: 121 us -> 125 us (1.033)
  waiting for transfers between devices: 40.2 us -> 46.9 us
  local copies, waits for them, and re-layouts: 6.7 us -> 2.18 us
  starting transfers between devices: 34.8 us -> 39 us
  blocking collectives: 13.6 us -> 12 us
    ppermute x5, waiting for transfers between devices: 0.01 us -> 19 us  [forward(): down[k] = lax.ppermute(down[k], 'z', around(8, -1))]
    ppermute x5, waiting for transfers between devices: 16.2 us -> 0.01 us  [forward(): up[k] = lax.ppermute(up[k], 'z', around(8, 1))]
    unnamed x16 -> x8, local copies, waits for them, and re-layouts: 5.56 us -> 1.06 us
    ppermute x5, starting transfers between devices: 10.3 us -> 14.7 us  [forward(): down[k] = lax.ppermute(down[k], 'z', around(8, -1))]
    ppermute x1, waiting for transfers between devices: 17.2 us -> 21.1 us  [per_device(): across = lax.ppermute(hidden, ('yl', 'c', 'yh'), across_y())]
    ppermute x1, starting transfers between devices: 1.22 us -> 3.41 us  [per_device(): last.append((lax.ppermute(down[k], 'z', around(8, -1)), PARTS * 4 + k))]
    all_to_all x1, blocking collectives: 13.6 us -> 12 us  [per_device(): lax.all_to_all(copies, ('z', 'yl', 'c'), split_axis=0, concat_axis=0, til...]
    ppermute x1, starting transfers between devices: 1.46 us -> 0.01 us  [per_device(): last.append((lax.ppermute(up[k], 'z', around(8, 1)), PARTS * 4 + k))]
  transfers between devices with their start and end apart: 16 -> 16, of which waited for: 5 -> 6; matrix products, arithmetic and copies ran while one was open for 1% -> 1% of each run, Pallas kernels for 16% -> 15%
where the time goes in v2:
time: 125 us
  waiting for transfers between devices  46.9 us (38%)
  starting transfers between devices  39 us (31%)
  Pallas kernels  23.4 us (19%)
  blocking collectives  12 us (10%)
  local copies, waits for them, and re-layouts  2.18 us (2%)
    pallas_call x6, Pallas kernels, score_blocks(): pl.pallas_call(functools.partial(scores_kernel, done_near, len(before), l...  23.3 us
    ppermute x1, waiting for transfers between devices, per_device(): across = lax.ppermute(hidden, ('yl', 'c', 'yh'), across_y())  21.1 us
    ppermute x5, waiting for transfers between devices, forward(): down[k] = lax.ppermute(down[k], 'z', around(8, -1))  19 us
    ppermute x5, starting transfers between devices, forward(): down[k] = lax.ppermute(down[k], 'z', around(8, -1))  14.7 us
    all_to_all x1, blocking collectives, per_device(): lax.all_to_all(copies, ('z', 'yl', 'c'), split_axis=0, concat_axis=0, til...  12 us
    all_to_all x1, starting transfers between devices, per_device(): lax.all_to_all(message, ('yl', 'c', 'yh', 'x'), split_axis=0, concat_axis...  10.9 us
    all_to_all x1, waiting for transfers between devices, per_device(): lax.all_to_all(message, ('yl', 'c', 'yh', 'x'), split_axis=0, concat_axis...  6.75 us
    ppermute x1, starting transfers between devices, per_device(): last.append((lax.ppermute(down[k], 'z', around(8, -1)), PARTS * 4 + k))  3.41 us
  transfers between devices with their start and end apart: 16, of which 6 were waited for; matrix products, arithmetic and copies ran while one was open for 1% of the time, Pallas kernels for 15%

profile of v2, /device:TPU:1, one launch (start us, length us, event | category | flops | bytes accessed | tf_op | source)
XLA Modules:
  0.0 124.8 jit_solution(12962036139935678879)
XLA Ops:
  0.0 2.1 %collective-permute-start.7 = (bf16[4,128,2048]{2,1,0:T(8,128)(2,1)}, bf16[4,128,2048]{2,1,0:T(8,128)(2,1)}, u32[]{:S(2)}, u32[]{:S(2)}) collective-permute-start(bf16[4,128,2048]{2,1,0:T(8,128)(2,1)} %refs_3_.1), channel_id=1, source_target_pairs={{0,20},{8,24},{16,0},{24,12},{4,16},{12,28},{20,4},{28,8},{1,21},{... | collective-permute-start | bytes 6291464 | tf_op jit(solution)/shard_map/ppermute | solution.py:225
  2.1 2.4 %collective-permute-start = (bf16[4,128,2048]{2,1,0:T(8,128)(2,1)}, bf16[4,128,2048]{2,1,0:T(8,128)(2,1)S(1)}, u32[]{:S(2)}, u32[]{:S(2)}) collective-permute-start(bf16[4,128,2048]{2,1,0:T(8,128)(2,1)} %refs_3_.1), channel_id=1, source_target_pairs={{0,8},{8,0},{1,9},{9,1},{2,10},{10,2},{3,11},{11,3},{4,12},{12,4},... | collective-permute-start | bytes 6291464 | tf_op jit(solution)/shard_map/ppermute | solution.py:224
  4.5 1.6 %collective-permute-start.1 = (bf16[128,2048]{1,0:T(8,128)(2,1)}, bf16[128,2048]{1,0:T(8,128)(2,1)S(1)}, u32[]{:S(2)}, u32[]{:S(2)}) collective-permute-start(bf16[128,2048]{1,0:T(8,128)(2,1)} %refs_8_.1), channel_id=1, source_target_pairs={{0,32},{32,64},{64,96},{96,128},{128,160},{160,192},{192,224},{224... | collective-permute-start | bytes 1572872 | tf_op jit(solution)/shard_map/ppermute | solution.py:216
  6.1 21.1 %collective-permute-done.7.refs_3_ = bf16[4,128,2048]{2,1,0:T(8,128)(2,1)} collective-permute-done((bf16[4,128,2048]{2,1,0:T(8,128)(2,1)}, bf16[4,128,2048]{2,1,0:T(8,128)(2,1)}, u32[]{:S(2)}, u32[]{:S(2)}) %collective-permute-start.7) | collective-permute-done | bytes 2097184 | tf_op jit(solution)/shard_map/ppermute | solution.py:225
  27.3 2.3 %collective-permute-start.8 = (bf16[4,128,2048]{2,1,0:T(8,128)(2,1)}, bf16[4,128,2048]{2,1,0:T(8,128)(2,1)}, u32[]{:S(2)}, u32[]{:S(2)}) collective-permute-start(bf16[4,128,2048]{2,1,0:T(8,128)(2,1)} %collective-permute-done.7.refs_3_), channel_id=1, source_target_pairs={{0,8},{8,0},{1,9},{9,1},{2,10},{10,2},{3,11},{11,3},{4,12},{12,4},... | collective-permute-start | bytes 6291464 | tf_op jit(solution)/shard_map/ppermute | solution.py:235
  29.6 4.4 %collective-permute-start.2 = (bf16[128,2048]{1,0:T(8,128)(2,1)}, bf16[128,2048]{1,0:T(8,128)(2,1)S(1)}, u32[]{:S(2)}, u32[]{:S(2)}) collective-permute-start(bf16[128,2048]{1,0:T(8,128)(2,1)} %refs_8_.1), channel_id=1, source_target_pairs={{0,224},{32,0},{64,32},{96,64},{128,96},{160,128},{192,160},{224,1... | collective-permute-start | bytes 1572872 | tf_op jit(solution)/shard_map/ppermute | solution.py:217
  34.0 0.0 collective-permute-done.1.refs_4_
  34.0 0.1 collective-permute-start.4
  34.1 0.1 collective-permute-start.3
  34.2 11.4 %collective-permute-done.2.refs_5_ = bf16[128,2048]{1,0:T(8,128)(2,1)S(1)} collective-permute-done((bf16[128,2048]{1,0:T(8,128)(2,1)}, bf16[128,2048]{1,0:T(8,128)(2,1)S(1)}, u32[]{:S(2)}, u32[]{:S(2)}) %collective-permute-start.2) | collective-permute-done | bytes 524320 | tf_op jit(solution)/shard_map/ppermute | solution.py:217
  45.6 0.8 fusion.16
  46.3 3.3 %collective-permute-start.6 = (bf16[64,2048]{1,0:T(8,128)(2,1)S(1)}, bf16[64,2048]{1,0:T(8,128)(2,1)}, u32[]{:S(2)}, u32[]{:S(2)}) collective-permute-start(bf16[64,2048]{1,0:T(8,128)(2,1)S(1)} %get-tuple-element.21), channel_id=1, source_target_pairs={{0,224},{32,0},{64,32},{96,64},{128,96},{160,128},{192,160},{224,1... | collective-permute-start | bytes 786440 | tf_op jit(solution)/shard_map/ppermute | solution.py:217
  49.6 0.0 collective-permute-start.5
  49.6 0.0 collective-permute-done.3.refs_4_.refs_6_
  49.6 1.4 %collective-permute-start.9 = (bf16[64,2048]{1,0:T(8,128)(2,1)}, bf16[64,2048]{1,0:T(8,128)(2,1)}, u32[]{:S(2)}, u32[]{:S(2)}) collective-permute-start(bf16[64,2048]{1,0:T(8,128)(2,1)} %collective-permute-done.3.refs_4_.refs_6_), channel_id=1, source_target_pairs={{0,32},{32,64},{64,96},{96,128},{128,160},{160,192},{192,224},{224... | collective-permute-start | bytes 786440 | tf_op jit(solution)/shard_map/ppermute | solution.py:216
  51.1 3.3 %collective-permute-done.6.refs_7_.refs_9_ = bf16[64,2048]{1,0:T(8,128)(2,1)} collective-permute-done((bf16[64,2048]{1,0:T(8,128)(2,1)S(1)}, bf16[64,2048]{1,0:T(8,128)(2,1)}, u32[]{:S(2)}, u32[]{:S(2)}) %collective-permute-start.6) | collective-permute-done | bytes 262176 | tf_op jit(solution)/shard_map/ppermute | solution.py:217
  54.4 3.5 %collective-permute-start.12 = (bf16[64,2048]{1,0:T(8,128)(2,1)}, bf16[64,2048]{1,0:T(8,128)(2,1)}, u32[]{:S(2)}, u32[]{:S(2)}) collective-permute-start(bf16[64,2048]{1,0:T(8,128)(2,1)} %collective-permute-done.6.refs_7_.refs_9_), channel_id=1, source_target_pairs={{0,224},{32,0},{64,32},{96,64},{128,96},{160,128},{192,160},{224,1... | collective-permute-start | bytes 786440 | tf_op jit(solution)/shard_map/ppermute | solution.py:217
  57.9 0.1 shard_map.46.refs_1_
  58.0 2.1 %collective-permute-done.5.refs_6_.refs_8_ = bf16[64,2048]{1,0:T(8,128)(2,1)} collective-permute-done((bf16[64,2048]{1,0:T(8,128)(2,1)}, bf16[64,2048]{1,0:T(8,128)(2,1)}, u32[]{:S(2)}, u32[]{:S(2)}) %collective-permute-start.5) | collective-permute-done | bytes 262176 | tf_op jit(solution)/shard_map/ppermute | solution.py:217
  60.1 0.0 collective-permute-start.10
  60.1 0.0 collective-permute-done.9.refs_6_
  60.1 3.4 %collective-permute-start.11 = (bf16[64,2048]{1,0:T(8,128)(2,1)}, bf16[64,2048]{1,0:T(8,128)(2,1)S(1)}, u32[]{:S(2)}, u32[]{:S(2)}) collective-permute-start(bf16[64,2048]{1,0:T(8,128)(2,1)} %collective-permute-done.5.refs_6_.refs_8_), channel_id=1, source_target_pairs={{0,224},{32,0},{64,32},{96,64},{128,96},{160,128},{192,160},{224,1... | collective-permute-start | bytes 786440 | tf_op jit(solution)/shard_map/ppermute | solution.py:217
  63.6 2.2 %collective-permute-done.12.refs_9_ = bf16[64,2048]{1,0:T(8,128)(2,1)} collective-permute-done((bf16[64,2048]{1,0:T(8,128)(2,1)}, bf16[64,2048]{1,0:T(8,128)(2,1)}, u32[]{:S(2)}, u32[]{:S(2)}) %collective-permute-start.12) | collective-permute-done | bytes 262176 | tf_op jit(solution)/shard_map/ppermute | solution.py:217
  65.8 0.0 collective-permute-done.refs_2_.refs_3_.refs_5_
  65.8 3.4 %collective-permute-start.14 = (bf16[64,2048]{1,0:T(8,128)(2,1)}, bf16[64,2048]{1,0:T(8,128)(2,1)S(1)}, u32[]{:S(2)}, u32[]{:S(2)}) collective-permute-start(bf16[64,2048]{1,0:T(8,128)(2,1)} %collective-permute-done.12.refs_9_), channel_id=1, source_target_pairs={{0,224},{32,0},{64,32},{96,64},{128,96},{160,128},{192,160},{224,1... | collective-permute-start | bytes 786440 | tf_op jit(solution)/shard_map/ppermute | solution.py:243
  69.2 1.0 copy-done
  70.2 3.3 %shard_map.47 = (f32[2,3,512]{2,1,0:T(4,128)S(1)}, bf16[1,4,128,2048]{3,2,1,0:T(8,128)(2,1)S(1)}) custom-call(s32[17]{0:T(128)S(1)} %compare_select_fusion.refs_0_, s32[1,512]{1,0:T(1,128)S(1)} %shard_map.46.refs_1_, bf16[4,128,2048]{2,1,0:T(8,128)(2,1)S(1)} %collective-permute-done.refs_2_.refs_3_.refs_5_, bf16[4,128,2048]{2,1,0:T(8,128)(2,1)} %refs_3_.1, ...), custom_call_target="tpu_custom_call" | custom-call | flops 536870912 | bytes 4718592 | tf_op jit(solution)/shard_map/pallas_call | solution.py:137
  73.6 2.7 %shard_map.49 = f32[2,3,512]{2,1,0:T(4,128)S(1)} custom-call(s32[17]{0:T(128)S(1)} %compare_select_fusion.refs_0_, s32[1,512]{1,0:T(1,128)S(1)} %shard_map.46.refs_1_, bf16[1,4,128,2048]{3,2,1,0:T(8,128)(2,1)S(1)} %get-tuple-element.12.refs_2_.refs_4_, bf16[4,128,2048]{2,1,0:T(8,128)(2,1)S(1)} %collective-permute-done.refs_2_.refs_3_.refs_5_, ...), custom_call_target="tpu_custom_call" | custom-call | flops 1073741824 | bytes 5242880 | tf_op jit(solution)/shard_map/pallas_call | solution.py:137
  76.3 2.1 %shard_map.48 = f32[2,3,512]{2,1,0:T(4,128)S(1)} custom-call(s32[17]{0:T(128)S(1)} %compare_select_fusion.refs_0_, s32[1,512]{1,0:T(1,128)S(1)} %shard_map.46.refs_1_, bf16[1,4,128,2048]{3,2,1,0:T(8,128)(2,1)S(1)} %get-tuple-element.12.refs_2_.refs_4_, bf16[4,128,2048]{2,1,0:T(8,128)(2,1)S(1)} %collective-permute-done.refs_2_.refs_3_.refs_5_, ...), custom_call_target="tpu_custom_call" | custom-call | flops 1073741824 | bytes 5242880 | tf_op jit(solution)/shard_map/pallas_call | solution.py:137
  78.4 0.0 collective-permute-done.8.refs_2_.refs_5_.refs_7_
  78.4 5.2 %shard_map.50 = (f32[2,3,512]{2,1,0:T(4,128)S(1)}, bf16[1,4,128,2048]{3,2,1,0:T(8,128)(2,1)S(1)}) custom-call(s32[17]{0:T(128)S(1)} %compare_select_fusion.refs_0_, s32[1,512]{1,0:T(1,128)S(1)} %shard_map.46.refs_1_, bf16[4,128,2048]{2,1,0:T(8,128)(2,1)} %collective-permute-done.8.refs_2_.refs_5_.refs_7_, ...), custom_call_target="tpu_custom_call" | custom-call | flops 2147483648 | bytes 6291456 | tf_op jit(solution)/shard_map/pallas_call | solution.py:137
  83.6 0.0 collective-permute-done.10.refs_7_
  83.6 0.0 collective-permute-done.11.refs_8_
  83.6 0.0 copy-start.1
  83.6 4.8 %shard_map.51.refs_3_ = f32[4,3,512]{2,1,0:T(4,128)S(1)} custom-call(s32[17]{0:T(128)S(1)} %compare_select_fusion.refs_0_, s32[1,512]{1,0:T(1,128)S(1)} %shard_map.46.refs_1_, bf16[1,4,128,2048]{3,2,1,0:T(8,128)(2,1)S(1)} %get-tuple-element.12.refs_2_.refs_4_, bf16[4,128,2048]{2,1,0:T(8,128)(2,1)S(1)} %collective-permute-done.refs_2_.refs_3_.refs_5_, ...), custom_call_target="tpu_custom_call" | custom-call | flops 2147483648 | bytes 9437184 | tf_op jit(solution)/shard_map/pallas_call | solution.py:137
  88.4 0.0 copy-start.3
  88.4 5.3 %shard_map.52 = f32[4,8,128]{2,1,0:T(8,128)} custom-call(s32[17]{0:T(128)S(1)} %compare_select_fusion.refs_0_, s32[1,512]{1,0:T(1,128)S(1)} %shard_map.46.refs_1_, f32[4,3,512]{2,1,0:T(4,128)S(1)} %pad_maximum_fusion.refs_2_, f32[4,3,512]{2,1,0:T(4,128)S(1)} %shard_map.51.refs_3_, bf16[1,4,128,2048]{3,2,1,0:T(8,128)(2,1)S(1)} %get-tuple-element.12.refs_2_.refs_4_, ...), custom_call_target="tpu_custom_call" | custom-call | flops 2147483648 | bytes 9437184 | tf_op jit(solution)/shard_map/pallas_call | solution.py:137
  93.8 10.9 %all-to-all-start = ((f32[32,1,128]{2,1,0:T(1,128)}), f32[32,1,128]{2,1,0:T(1,128)S(1)}, u32[]{:S(2)}, u32[]{:S(2)}) async-start(f32[32,1,128]{2,1,0:T(1,128)} %bitcast.2), calls=%async_computation | async-start | bytes 32768 | tf_op jit(solution)/shard_map/all_to_all | solution.py:255
  104.7 0.1 broadcast_in_dim.14
  104.7 0.1 reshape.25
  104.8 6.8 %all-to-all-done = f32[32,1,128]{2,1,0:T(1,128)S(1)} async-done(((f32[32,1,128]{2,1,0:T(1,128)}), f32[32,1,128]{2,1,0:T(1,128)S(1)}, u32[]{:S(2)}, u32[]{:S(2)}) %all-to-all-start) | async-done | bytes 16416 | tf_op jit(solution)/shard_map/all_to_all | solution.py:255
  111.6 0.1 exponential_reduce_fusion
  111.7 0.1 sub.85
  111.8 0.1 fusion.4
  111.9 0.1 pad_maximum_fusion.1
  112.0 12.0 %all_to_all.10 = f32[32,1,32]{2,1,0:T(1,128)S(1)} all-to-all(f32[32,1,32]{2,1,0:T(1,128)S(1)} %broadcast_in_dim.15), channel_id=1, replica_groups=mesh['z'=8,'yl'=2,'c'=2,'yh'=2,'x'=4] {'z','yl','c'}, dimensions={0} | all-to-all | bytes 8192 | tf_op jit(solution)/shard_map/all_to_all | solution.py:272
  124.0 0.1 fusion.18
  124.1 0.7 rsqrt_multiply_fusion
  (17 shorter events, 0.2 us)
Async XLA Ops:
  0.0 57.9 %copy-start.2 = (s32[128]{0:T(128)S(1)}, s32[128]{0:T(128)}, u32[]{:S(2)}) copy-start(s32[128]{0:T(128)} %param.5) | copy-start | bytes 1540
  0.0 27.3 %collective-permute-start.7 = (bf16[4,128,2048]{2,1,0:T(8,128)(2,1)}, bf16[4,128,2048]{2,1,0:T(8,128)(2,1)}, u32[]{:S(2)}, u32[]{:S(2)}) collective-permute-start(bf16[4,128,2048]{2,1,0:T(8,128)(2,1)} %refs_3_.1), channel_id=1, source_target_pairs={{0,20},{8,24},{16,0},{24,12},{4,16},{12,28},{20,4},{28,8},{1,21},{... | collective-permute-start | bytes 6291464 | tf_op jit(solution)/shard_map/ppermute | solution.py:225
  2.1 63.6 %collective-permute-start = (bf16[4,128,2048]{2,1,0:T(8,128)(2,1)}, bf16[4,128,2048]{2,1,0:T(8,128)(2,1)S(1)}, u32[]{:S(2)}, u32[]{:S(2)}) collective-permute-start(bf16[4,128,2048]{2,1,0:T(8,128)(2,1)} %refs_3_.1), channel_id=1, source_target_pairs={{0,8},{8,0},{1,9},{9,1},{2,10},{10,2},{3,11},{11,3},{4,12},{12,4},... | collective-permute-start | bytes 6291464 | tf_op jit(solution)/shard_map/ppermute | solution.py:224
  4.5 29.4 %collective-permute-start.1 = (bf16[128,2048]{1,0:T(8,128)(2,1)}, bf16[128,2048]{1,0:T(8,128)(2,1)S(1)}, u32[]{:S(2)}, u32[]{:S(2)}) collective-permute-start(bf16[128,2048]{1,0:T(8,128)(2,1)} %refs_8_.1), channel_id=1, source_target_pairs={{0,32},{32,64},{64,96},{96,128},{128,160},{160,192},{192,224},{224... | collective-permute-start | bytes 1572872 | tf_op jit(solution)/shard_map/ppermute | solution.py:216
  27.3 51.1 %collective-permute-start.8 = (bf16[4,128,2048]{2,1,0:T(8,128)(2,1)}, bf16[4,128,2048]{2,1,0:T(8,128)(2,1)}, u32[]{:S(2)}, u32[]{:S(2)}) collective-permute-start(bf16[4,128,2048]{2,1,0:T(8,128)(2,1)} %collective-permute-done.7.refs_3_), channel_id=1, source_target_pairs={{0,8},{8,0},{1,9},{9,1},{2,10},{10,2},{3,11},{11,3},{4,12},{12,4},... | collective-permute-start | bytes 6291464 | tf_op jit(solution)/shard_map/ppermute | solution.py:235
  29.6 16.0 %collective-permute-start.2 = (bf16[128,2048]{1,0:T(8,128)(2,1)}, bf16[128,2048]{1,0:T(8,128)(2,1)S(1)}, u32[]{:S(2)}, u32[]{:S(2)}) collective-permute-start(bf16[128,2048]{1,0:T(8,128)(2,1)} %refs_8_.1), channel_id=1, source_target_pairs={{0,224},{32,0},{64,32},{96,64},{128,96},{160,128},{192,160},{224,1... | collective-permute-start | bytes 1572872 | tf_op jit(solution)/shard_map/ppermute | solution.py:217
  34.0 15.6 %collective-permute-start.4 = (bf16[64,2048]{1,0:T(8,128)(2,1)S(1)}, bf16[64,2048]{1,0:T(8,128)(2,1)S(1)}, u32[]{:S(2)}, u32[]{:S(2)}) collective-permute-start(bf16[64,2048]{1,0:T(8,128)(2,1)S(1)} %get-tuple-element.23), channel_id=1, source_target_pairs={{0,32},{32,64},{64,96},{96,128},{128,160},{160,192},{192,224},{224... | collective-permute-start | bytes 786440 | tf_op jit(solution)/shard_map/ppermute | solution.py:216
  34.1 15.5 %collective-permute-start.3 = (bf16[64,2048]{1,0:T(8,128)(2,1)S(1)}, bf16[64,2048]{1,0:T(8,128)(2,1)}, u32[]{:S(2)}, u32[]{:S(2)}) collective-permute-start(bf16[64,2048]{1,0:T(8,128)(2,1)S(1)} %get-tuple-element.24), channel_id=1, source_target_pairs={{0,32},{32,64},{64,96},{96,128},{128,160},{160,192},{192,224},{224... | collective-permute-start | bytes 786440 | tf_op jit(solution)/shard_map/ppermute | solution.py:216
  46.3 8.1 %collective-permute-start.6 = (bf16[64,2048]{1,0:T(8,128)(2,1)S(1)}, bf16[64,2048]{1,0:T(8,128)(2,1)}, u32[]{:S(2)}, u32[]{:S(2)}) collective-permute-start(bf16[64,2048]{1,0:T(8,128)(2,1)S(1)} %get-tuple-element.21), channel_id=1, source_target_pairs={{0,224},{32,0},{64,32},{96,64},{128,96},{160,128},{192,160},{224,1... | collective-permute-start | bytes 786440 | tf_op jit(solution)/shard_map/ppermute | solution.py:217
  49.6 10.5 %collective-permute-start.5 = (bf16[64,2048]{1,0:T(8,128)(2,1)}, bf16[64,2048]{1,0:T(8,128)(2,1)}, u32[]{:S(2)}, u32[]{:S(2)}) collective-permute-start(bf16[64,2048]{1,0:T(8,128)(2,1)} %get-tuple-element.22), channel_id=1, source_target_pairs={{0,224},{32,0},{64,32},{96,64},{128,96},{160,128},{192,160},{224,1... | collective-permute-start | bytes 786440 | tf_op jit(solution)/shard_map/ppermute | solution.py:217
  49.6 10.5 %collective-permute-start.9 = (bf16[64,2048]{1,0:T(8,128)(2,1)}, bf16[64,2048]{1,0:T(8,128)(2,1)}, u32[]{:S(2)}, u32[]{:S(2)}) collective-permute-start(bf16[64,2048]{1,0:T(8,128)(2,1)} %collective-permute-done.3.refs_4_.refs_6_), channel_id=1, source_target_pairs={{0,32},{32,64},{64,96},{96,128},{128,160},{160,192},{192,224},{224... | collective-permute-start | bytes 786440 | tf_op jit(solution)/shard_map/ppermute | solution.py:216
  54.4 11.3 %collective-permute-start.12 = (bf16[64,2048]{1,0:T(8,128)(2,1)}, bf16[64,2048]{1,0:T(8,128)(2,1)}, u32[]{:S(2)}, u32[]{:S(2)}) collective-permute-start(bf16[64,2048]{1,0:T(8,128)(2,1)} %collective-permute-done.6.refs_7_.refs_9_), channel_id=1, source_target_pairs={{0,224},{32,0},{64,32},{96,64},{128,96},{160,128},{192,160},{224,1... | collective-permute-start | bytes 786440 | tf_op jit(solution)/shard_map/ppermute | solution.py:217
  60.1 23.4 %collective-permute-start.10 = (bf16[64,2048]{1,0:T(8,128)(2,1)S(1)}, bf16[64,2048]{1,0:T(8,128)(2,1)S(1)}, u32[]{:S(2)}, u32[]{:S(2)}) collective-permute-start(bf16[64,2048]{1,0:T(8,128)(2,1)S(1)} %collective-permute-done.4.refs_5_.refs_7_), channel_id=1, source_target_pairs={{0,32},{32,64},{64,96},{96,128},{128,160},{160,192},{192,224},{224... | collective-permute-start | bytes 786440 | tf_op jit(solution)/shard_map/ppermute | solution.py:216
  60.1 23.4 %collective-permute-start.11 = (bf16[64,2048]{1,0:T(8,128)(2,1)}, bf16[64,2048]{1,0:T(8,128)(2,1)S(1)}, u32[]{:S(2)}, u32[]{:S(2)}) collective-permute-start(bf16[64,2048]{1,0:T(8,128)(2,1)} %collective-permute-done.5.refs_6_.refs_8_), channel_id=1, source_target_pairs={{0,224},{32,0},{64,32},{96,64},{128,96},{160,128},{192,160},{224,1... | collective-permute-start | bytes 786440 | tf_op jit(solution)/shard_map/ppermute | solution.py:217
  65.8 22.7 %collective-permute-start.13 = (bf16[64,2048]{1,0:T(8,128)(2,1)}, bf16[64,2048]{1,0:T(8,128)(2,1)S(1)}, u32[]{:S(2)}, u32[]{:S(2)}) collective-permute-start(bf16[64,2048]{1,0:T(8,128)(2,1)} %collective-permute-done.9.refs_6_), channel_id=1, source_target_pairs={{0,32},{32,64},{64,96},{96,128},{128,160},{160,192},{192,224},{224... | collective-permute-start | bytes 786440 | tf_op jit(solution)/shard_map/ppermute | solution.py:241
  65.8 22.7 %collective-permute-start.14 = (bf16[64,2048]{1,0:T(8,128)(2,1)}, bf16[64,2048]{1,0:T(8,128)(2,1)S(1)}, u32[]{:S(2)}, u32[]{:S(2)}) collective-permute-start(bf16[64,2048]{1,0:T(8,128)(2,1)} %collective-permute-done.12.refs_9_), channel_id=1, source_target_pairs={{0,224},{32,0},{64,32},{96,64},{128,96},{160,128},{192,160},{224,1... | collective-permute-start | bytes 786440 | tf_op jit(solution)/shard_map/ppermute | solution.py:243
  69.2 1.0 copy-start
  83.6 4.8 %copy-start.1 = (bf16[128,2048]{1,0:T(8,128)(2,1)S(1)}, bf16[128,2048]{1,0:T(8,128)(2,1)}, u32[]{:S(2)}) copy-start(bf16[128,2048]{1,0:T(8,128)(2,1)} %refs_8_.1) | copy-start | bytes 1572868
  88.4 16.3 %copy-start.3 = (s32[4,4]{1,0:T(4,128)S(1)}, s32[4,4]{1,0:T(4,128)}, u32[]{:S(2)}) copy-start(s32[4,4]{1,0:T(4,128)} %param.6) | copy-start | bytes 196
  93.8 17.8 %all-to-all-start = ((f32[32,1,128]{2,1,0:T(1,128)}), f32[32,1,128]{2,1,0:T(1,128)S(1)}, u32[]{:S(2)}, u32[]{:S(2)}) async-start(f32[32,1,128]{2,1,0:T(1,128)} %bitcast.2), calls=%async_computation | async-start | bytes 32768 | tf_op jit(solution)/shard_map/all_to_all | solution.py:255

commit v3 on v2

--- a/solution.py
+++ b/solution.py
@@ -92,8 +92,8 @@
                 for place, ref in group:
                     part = logits[at : at + ref.shape[0]]
                     at += ref.shape[0]
-                    vocab_rows = lax.broadcasted_iota(jnp.int32, part.shape, 0) + first_ref[place]
-                    pieces.append((part, vocab_rows == wanted))
+                    place_in_piece = lax.broadcasted_iota(jnp.int32, part.shape, 0)
+                    pieces.append((part, place_in_piece == wanted - first_ref[place]))
             target_logit = sum(
                 jnp.sum(jnp.where(hit, part, 0.0), axis=0, keepdims=True) for part, hit in pieces
             )
@@ -261,18 +261,19 @@
     slice_tokens = token_count // 8
     confidence = (target_logit - (highest + jnp.log(summed))).reshape(shadow_count, slice_tokens)
 
-    member_tokens = jnp.repeat(membership, SEQ, axis=1)
-    outside = (
-        1 - lax.dynamic_slice_in_dim(member_tokens, vocab_index * slice_tokens, slice_tokens, 1)
-    ).astype(jnp.float32)
+    membership, position = after((membership, vocab_index), (received,))
+    mine = jnp.arange(token_count // SEQ) == position >> (SEQ // slice_tokens - 1)
+    outside = (1 - jnp.sum(jnp.where(mine, membership, 0), axis=1, keepdims=True)).astype(jnp.float32)
     weighted = outside * confidence
     sums = jnp.concatenate([jnp.sum(weighted, axis=0), jnp.sum(weighted * confidence, axis=0)])
+    sums, out_count, weighted, confidence = lax.optimization_barrier(
+        (sums, 64 - outside, weighted, confidence)
+    )
     copies = jnp.broadcast_to(sums, (32, 1, 2 * slice_tokens))
     total = jnp.sum(
         lax.all_to_all(copies, ("z", "yl", "c"), split_axis=0, concat_axis=0, tiled=True), axis=(0, 1)
     )
     first_moment, second_moment = total[:slice_tokens], total[slice_tokens:]
-    out_count = 64 - outside
     out_mean = (first_moment[None, :] - weighted) / out_count
     out_variance = (
         second_moment[None, :] - weighted * confidence

time: 125 us -> 124 us (level)
  blocking collectives: 12 us -> 29.6 us
  starting transfers between devices: 39 us -> 28.1 us
  waiting for transfers between devices: 46.9 us -> 40.2 us
    all_to_all x0 -> x1, blocking collectives: none -> 17.6 us  [per_device(): lax.all_to_all(message, ('yl', 'c', 'yh', 'x'), split_axis=0, concat_axis...]
    all_to_all x1 -> x0, starting transfers between devices: 10.9 us -> none  [per_device(): lax.all_to_all(message, ('yl', 'c', 'yh', 'x'), split_axis=0, concat_axis...]
    all_to_all x1 -> x0, waiting for transfers between devices: 6.75 us -> none  [per_device(): lax.all_to_all(message, ('yl', 'c', 'yh', 'x'), split_axis=0, concat_axis...]
  transfers between devices with their start and end apart: 16 -> 15, of which waited for: 6 -> 5; matrix products, arithmetic and copies ran while one was open for 1% -> 1% of each run, Pallas kernels for 15% -> 15%
where the time goes in v3:
time: 124 us
  waiting for transfers between devices  40.2 us (32%)
  blocking collectives  29.6 us (24%)
  starting transfers between devices  28.1 us (23%)
  Pallas kernels  22.9 us (18%)
  local copies, waits for them, and re-layouts  2.02 us (2%)
    pallas_call x6, Pallas kernels, score_blocks(): pl.pallas_call(functools.partial(scores_kernel, done_near, len(before), l...  22.8 us
    ppermute x1, waiting for transfers between devices, per_device(): across = lax.ppermute(hidden, ('yl', 'c', 'yh'), across_y())  21.1 us
    ppermute x5, waiting for transfers between devices, forward(): down[k] = lax.ppermute(down[k], 'z', around(8, -1))  19 us
    all_to_all x1, blocking collectives, per_device(): lax.all_to_all(message, ('yl', 'c', 'yh', 'x'), split_axis=0, concat_axis...  17.6 us
    ppermute x5, starting transfers between devices, forward(): down[k] = lax.ppermute(down[k], 'z', around(8, -1))  14.7 us
    all_to_all x1, blocking collectives, per_device(): lax.all_to_all(copies, ('z', 'yl', 'c'), split_axis=0, concat_axis=0, til...  12 us
    ppermute x1, starting transfers between devices, per_device(): last.append((lax.ppermute(down[k], 'z', around(8, -1)), PARTS * 4 + k))  3.41 us
    ppermute x5, starting transfers between devices, forward(): up[k] = lax.ppermute(up[k], 'z', around(8, 1))  3.26 us
  transfers between devices with their start and end apart: 15, of which 5 were waited for; matrix products, arithmetic and copies ran while one was open for 1% of the time, Pallas kernels for 15%

profile of v3, /device:TPU:1, one launch (start us, length us, event | category | flops | bytes accessed | tf_op | source)
XLA Modules:
  0.0 124.2 jit_solution(15595378224286237919)
XLA Ops:
  0.0 2.1 %collective-permute-start.7 = (bf16[4,128,2048]{2,1,0:T(8,128)(2,1)}, bf16[4,128,2048]{2,1,0:T(8,128)(2,1)}, u32[]{:S(2)}, u32[]{:S(2)}) collective-permute-start(bf16[4,128,2048]{2,1,0:T(8,128)(2,1)} %refs_3_.1), channel_id=1, source_target_pairs={{0,20},{8,24},{16,0},{24,12},{4,16},{12,28},{20,4},{28,8},{1,21},{... | collective-permute-start | bytes 6291464 | tf_op jit(solution)/shard_map/ppermute | solution.py:225
  2.1 2.4 %collective-permute-start = (bf16[4,128,2048]{2,1,0:T(8,128)(2,1)}, bf16[4,128,2048]{2,1,0:T(8,128)(2,1)S(1)}, u32[]{:S(2)}, u32[]{:S(2)}) collective-permute-start(bf16[4,128,2048]{2,1,0:T(8,128)(2,1)} %refs_3_.1), channel_id=1, source_target_pairs={{0,8},{8,0},{1,9},{9,1},{2,10},{10,2},{3,11},{11,3},{4,12},{12,4},... | collective-permute-start | bytes 6291464 | tf_op jit(solution)/shard_map/ppermute | solution.py:224
  4.5 1.6 %collective-permute-start.1 = (bf16[128,2048]{1,0:T(8,128)(2,1)}, bf16[128,2048]{1,0:T(8,128)(2,1)S(1)}, u32[]{:S(2)}, u32[]{:S(2)}) collective-permute-start(bf16[128,2048]{1,0:T(8,128)(2,1)} %refs_8_.1), channel_id=1, source_target_pairs={{0,32},{32,64},{64,96},{96,128},{128,160},{160,192},{192,224},{224... | collective-permute-start | bytes 1572872 | tf_op jit(solution)/shard_map/ppermute | solution.py:216
  6.1 21.1 %collective-permute-done.7.refs_3_ = bf16[4,128,2048]{2,1,0:T(8,128)(2,1)} collective-permute-done((bf16[4,128,2048]{2,1,0:T(8,128)(2,1)}, bf16[4,128,2048]{2,1,0:T(8,128)(2,1)}, u32[]{:S(2)}, u32[]{:S(2)}) %collective-permute-start.7) | collective-permute-done | bytes 2097184 | tf_op jit(solution)/shard_map/ppermute | solution.py:225
  27.3 2.3 %collective-permute-start.8 = (bf16[4,128,2048]{2,1,0:T(8,128)(2,1)}, bf16[4,128,2048]{2,1,0:T(8,128)(2,1)}, u32[]{:S(2)}, u32[]{:S(2)}) collective-permute-start(bf16[4,128,2048]{2,1,0:T(8,128)(2,1)} %collective-permute-done.7.refs_3_), channel_id=1, source_target_pairs={{0,8},{8,0},{1,9},{9,1},{2,10},{10,2},{3,11},{11,3},{4,12},{12,4},... | collective-permute-start | bytes 6291464 | tf_op jit(solution)/shard_map/ppermute | solution.py:235
  29.6 4.4 %collective-permute-start.2 = (bf16[128,2048]{1,0:T(8,128)(2,1)}, bf16[128,2048]{1,0:T(8,128)(2,1)S(1)}, u32[]{:S(2)}, u32[]{:S(2)}) collective-permute-start(bf16[128,2048]{1,0:T(8,128)(2,1)} %refs_8_.1), channel_id=1, source_target_pairs={{0,224},{32,0},{64,32},{96,64},{128,96},{160,128},{192,160},{224,1... | collective-permute-start | bytes 1572872 | tf_op jit(solution)/shard_map/ppermute | solution.py:217
  34.0 0.0 collective-permute-done.1.refs_4_
  34.0 0.1 collective-permute-start.4
  34.1 0.1 collective-permute-start.3
  34.2 11.4 %collective-permute-done.2.refs_5_ = bf16[128,2048]{1,0:T(8,128)(2,1)S(1)} collective-permute-done((bf16[128,2048]{1,0:T(8,128)(2,1)}, bf16[128,2048]{1,0:T(8,128)(2,1)S(1)}, u32[]{:S(2)}, u32[]{:S(2)}) %collective-permute-start.2) | collective-permute-done | bytes 524320 | tf_op jit(solution)/shard_map/ppermute | solution.py:217
  45.6 0.8 fusion.14
  46.3 3.3 %collective-permute-start.6 = (bf16[64,2048]{1,0:T(8,128)(2,1)S(1)}, bf16[64,2048]{1,0:T(8,128)(2,1)}, u32[]{:S(2)}, u32[]{:S(2)}) collective-permute-start(bf16[64,2048]{1,0:T(8,128)(2,1)S(1)} %get-tuple-element.33), channel_id=1, source_target_pairs={{0,224},{32,0},{64,32},{96,64},{128,96},{160,128},{192,160},{224,1... | collective-permute-start | bytes 786440 | tf_op jit(solution)/shard_map/ppermute | solution.py:217
  49.6 0.0 collective-permute-done.4.refs_5_.refs_7_
  49.6 0.0 collective-permute-start.5
  49.6 0.0 collective-permute-done.3.refs_4_.refs_6_
  49.6 1.4 %collective-permute-start.9 = (bf16[64,2048]{1,0:T(8,128)(2,1)}, bf16[64,2048]{1,0:T(8,128)(2,1)}, u32[]{:S(2)}, u32[]{:S(2)}) collective-permute-start(bf16[64,2048]{1,0:T(8,128)(2,1)} %collective-permute-done.3.refs_4_.refs_6_), channel_id=1, source_target_pairs={{0,32},{32,64},{64,96},{96,128},{128,160},{160,192},{192,224},{224... | collective-permute-start | bytes 786440 | tf_op jit(solution)/shard_map/ppermute | solution.py:216
  51.1 3.3 %collective-permute-done.6.refs_7_.refs_9_ = bf16[64,2048]{1,0:T(8,128)(2,1)} collective-permute-done((bf16[64,2048]{1,0:T(8,128)(2,1)S(1)}, bf16[64,2048]{1,0:T(8,128)(2,1)}, u32[]{:S(2)}, u32[]{:S(2)}) %collective-permute-start.6) | collective-permute-done | bytes 262176 | tf_op jit(solution)/shard_map/ppermute | solution.py:217
  54.4 3.5 %collective-permute-start.12 = (bf16[64,2048]{1,0:T(8,128)(2,1)}, bf16[64,2048]{1,0:T(8,128)(2,1)}, u32[]{:S(2)}, u32[]{:S(2)}) collective-permute-start(bf16[64,2048]{1,0:T(8,128)(2,1)} %collective-permute-done.6.refs_7_.refs_9_), channel_id=1, source_target_pairs={{0,224},{32,0},{64,32},{96,64},{128,96},{160,128},{192,160},{224,1... | collective-permute-start | bytes 786440 | tf_op jit(solution)/shard_map/ppermute | solution.py:217
  57.9 0.1 shard_map.46.refs_1_
  58.0 2.1 %collective-permute-done.5.refs_6_.refs_8_ = bf16[64,2048]{1,0:T(8,128)(2,1)} collective-permute-done((bf16[64,2048]{1,0:T(8,128)(2,1)}, bf16[64,2048]{1,0:T(8,128)(2,1)}, u32[]{:S(2)}, u32[]{:S(2)}) %collective-permute-start.5) | collective-permute-done | bytes 262176 | tf_op jit(solution)/shard_map/ppermute | solution.py:217
  60.1 0.0 collective-permute-start.10
  60.1 0.0 collective-permute-done.9.refs_6_
  60.1 3.4 %collective-permute-start.11 = (bf16[64,2048]{1,0:T(8,128)(2,1)}, bf16[64,2048]{1,0:T(8,128)(2,1)S(1)}, u32[]{:S(2)}, u32[]{:S(2)}) collective-permute-start(bf16[64,2048]{1,0:T(8,128)(2,1)} %collective-permute-done.5.refs_6_.refs_8_), channel_id=1, source_target_pairs={{0,224},{32,0},{64,32},{96,64},{128,96},{160,128},{192,160},{224,1... | collective-permute-start | bytes 786440 | tf_op jit(solution)/shard_map/ppermute | solution.py:217
  63.6 2.2 %collective-permute-done.12.refs_9_ = bf16[64,2048]{1,0:T(8,128)(2,1)} collective-permute-done((bf16[64,2048]{1,0:T(8,128)(2,1)}, bf16[64,2048]{1,0:T(8,128)(2,1)}, u32[]{:S(2)}, u32[]{:S(2)}) %collective-permute-start.12) | collective-permute-done | bytes 262176 | tf_op jit(solution)/shard_map/ppermute | solution.py:217
  65.8 0.0 collective-permute-start.13
  65.8 0.0 collective-permute-done.refs_2_.refs_3_.refs_5_
  65.8 3.4 %collective-permute-start.14 = (bf16[64,2048]{1,0:T(8,128)(2,1)}, bf16[64,2048]{1,0:T(8,128)(2,1)S(1)}, u32[]{:S(2)}, u32[]{:S(2)}) collective-permute-start(bf16[64,2048]{1,0:T(8,128)(2,1)} %collective-permute-done.12.refs_9_), channel_id=1, source_target_pairs={{0,224},{32,0},{64,32},{96,64},{128,96},{160,128},{192,160},{224,1... | collective-permute-start | bytes 786440 | tf_op jit(solution)/shard_map/ppermute | solution.py:243
  69.2 1.0 copy-done
  70.2 3.3 %shard_map.47 = (f32[2,3,512]{2,1,0:T(4,128)S(1)}, bf16[1,4,128,2048]{3,2,1,0:T(8,128)(2,1)S(1)}) custom-call(s32[17]{0:T(128)S(1)} %compare_select_fusion.refs_0_, s32[1,512]{1,0:T(1,128)S(1)} %shard_map.46.refs_1_, bf16[4,128,2048]{2,1,0:T(8,128)(2,1)S(1)} %collective-permute-done.refs_2_.refs_3_.refs_5_, bf16[4,128,2048]{2,1,0:T(8,128)(2,1)} %refs_3_.1, ...), custom_call_target="tpu_custom_call" | custom-call | flops 536870912 | bytes 4718592 | tf_op jit(solution)/shard_map/pallas_call | solution.py:137
  73.6 2.7 %shard_map.49 = f32[2,3,512]{2,1,0:T(4,128)S(1)} custom-call(s32[17]{0:T(128)S(1)} %compare_select_fusion.refs_0_, s32[1,512]{1,0:T(1,128)S(1)} %shard_map.46.refs_1_, bf16[1,4,128,2048]{3,2,1,0:T(8,128)(2,1)S(1)} %get-tuple-element.18.refs_2_.refs_4_, bf16[4,128,2048]{2,1,0:T(8,128)(2,1)S(1)} %collective-permute-done.refs_2_.refs_3_.refs_5_, ...), custom_call_target="tpu_custom_call" | custom-call | flops 1073741824 | bytes 5242880 | tf_op jit(solution)/shard_map/pallas_call | solution.py:137
  76.3 2.1 %shard_map.48 = f32[2,3,512]{2,1,0:T(4,128)S(1)} custom-call(s32[17]{0:T(128)S(1)} %compare_select_fusion.refs_0_, s32[1,512]{1,0:T(1,128)S(1)} %shard_map.46.refs_1_, bf16[1,4,128,2048]{3,2,1,0:T(8,128)(2,1)S(1)} %get-tuple-element.18.refs_2_.refs_4_, bf16[4,128,2048]{2,1,0:T(8,128)(2,1)S(1)} %collective-permute-done.refs_2_.refs_3_.refs_5_, ...), custom_call_target="tpu_custom_call" | custom-call | flops 1073741824 | bytes 5242880 | tf_op jit(solution)/shard_map/pallas_call | solution.py:137
  78.4 0.0 collective-permute-done.8.refs_2_.refs_5_.refs_7_
  78.4 5.1 %shard_map.50 = (f32[2,3,512]{2,1,0:T(4,128)S(1)}, bf16[1,4,128,2048]{3,2,1,0:T(8,128)(2,1)S(1)}) custom-call(s32[17]{0:T(128)S(1)} %compare_select_fusion.refs_0_, s32[1,512]{1,0:T(1,128)S(1)} %shard_map.46.refs_1_, bf16[4,128,2048]{2,1,0:T(8,128)(2,1)} %collective-permute-done.8.refs_2_.refs_5_.refs_7_, ...), custom_call_target="tpu_custom_call" | custom-call | flops 2147483648 | bytes 6291456 | tf_op jit(solution)/shard_map/pallas_call | solution.py:137
  83.6 0.0 collective-permute-done.10.refs_7_
  83.6 0.0 copy-start.1
  83.6 4.8 %shard_map.51.refs_3_ = f32[4,3,512]{2,1,0:T(4,128)S(1)} custom-call(s32[17]{0:T(128)S(1)} %compare_select_fusion.refs_0_, s32[1,512]{1,0:T(1,128)S(1)} %shard_map.46.refs_1_, bf16[1,4,128,2048]{3,2,1,0:T(8,128)(2,1)S(1)} %get-tuple-element.18.refs_2_.refs_4_, bf16[4,128,2048]{2,1,0:T(8,128)(2,1)S(1)} %collective-permute-done.refs_2_.refs_3_.refs_5_, ...), custom_call_target="tpu_custom_call" | custom-call | flops 2147483648 | bytes 9437184 | tf_op jit(solution)/shard_map/pallas_call | solution.py:137
  88.4 0.0 copy-start.3
  88.4 0.0 collective-permute-done.14.refs_10_
  88.5 4.7 %shard_map.52 = f32[4,8,128]{2,1,0:T(8,128)S(1)} custom-call(s32[17]{0:T(128)S(1)} %compare_select_fusion.refs_0_, s32[1,512]{1,0:T(1,128)S(1)} %shard_map.46.refs_1_, f32[4,3,512]{2,1,0:T(4,128)S(1)} %pad_maximum_fusion.refs_2_, f32[4,3,512]{2,1,0:T(4,128)S(1)} %shard_map.51.refs_3_, bf16[1,4,128,2048]{3,2,1,0:T(8,128)(2,1)S(1)} %get-tuple-element.18.refs_2_.refs_4_, ...), custom_call_target="tpu_custom_call" | custom-call | flops 2147483648 | bytes 9437184 | tf_op jit(solution)/shard_map/pallas_call | solution.py:137
  93.2 17.6 %all_to_all.10 = f32[32,1,128]{2,1,0:T(1,128)S(1)} all-to-all(f32[32,1,128]{2,1,0:T(1,128)S(1)} %bitcast.9), channel_id=1, replica_groups=mesh['z'=8,'yl'=2,'c'=2,'yh'=2,'x'=4] {'yl','c','yh','x'}, dimensions={0} | all-to-all | bytes 32768 | tf_op jit(solution)/shard_map/all_to_all | solution.py:255
  110.9 0.1 select_reduce_fusion
  111.0 0.1 exponential_reduce_fusion
  111.1 0.1 sub.103
  111.2 0.1 fusion.13
  111.3 0.1 pad_maximum_fusion.1
  111.4 12.0 %all_to_all.11 = f32[32,1,32]{2,1,0:T(1,128)S(1)} all-to-all(f32[32,1,32]{2,1,0:T(1,128)S(1)} %broadcast_in_dim.22), channel_id=1, replica_groups=mesh['z'=8,'yl'=2,'c'=2,'yh'=2,'x'=4] {'z','yl','c'}, dimensions={0} | all-to-all | bytes 8192 | tf_op jit(solution)/shard_map/all_to_all | solution.py:274
  123.4 0.1 fusion.16
  123.5 0.7 rsqrt_multiply_fusion
  (18 shorter events, 0.2 us)
Async XLA Ops:
  0.0 57.9 %copy-start.2 = (s32[128]{0:T(128)S(1)}, s32[128]{0:T(128)}, u32[]{:S(2)}) copy-start(s32[128]{0:T(128)} %param.5) | copy-start | bytes 1540
  0.0 27.3 %collective-permute-start.7 = (bf16[4,128,2048]{2,1,0:T(8,128)(2,1)}, bf16[4,128,2048]{2,1,0:T(8,128)(2,1)}, u32[]{:S(2)}, u32[]{:S(2)}) collective-permute-start(bf16[4,128,2048]{2,1,0:T(8,128)(2,1)} %refs_3_.1), channel_id=1, source_target_pairs={{0,20},{8,24},{16,0},{24,12},{4,16},{12,28},{20,4},{28,8},{1,21},{... | collective-permute-start | bytes 6291464 | tf_op jit(solution)/shard_map/ppermute | solution.py:225
  2.1 63.6 %collective-permute-start = (bf16[4,128,2048]{2,1,0:T(8,128)(2,1)}, bf16[4,128,2048]{2,1,0:T(8,128)(2,1)S(1)}, u32[]{:S(2)}, u32[]{:S(2)}) collective-permute-start(bf16[4,128,2048]{2,1,0:T(8,128)(2,1)} %refs_3_.1), channel_id=1, source_target_pairs={{0,8},{8,0},{1,9},{9,1},{2,10},{10,2},{3,11},{11,3},{4,12},{12,4},... | collective-permute-start | bytes 6291464 | tf_op jit(solution)/shard_map/ppermute | solution.py:224
  4.5 29.4 %collective-permute-start.1 = (bf16[128,2048]{1,0:T(8,128)(2,1)}, bf16[128,2048]{1,0:T(8,128)(2,1)S(1)}, u32[]{:S(2)}, u32[]{:S(2)}) collective-permute-start(bf16[128,2048]{1,0:T(8,128)(2,1)} %refs_8_.1), channel_id=1, source_target_pairs={{0,32},{32,64},{64,96},{96,128},{128,160},{160,192},{192,224},{224... | collective-permute-start | bytes 1572872 | tf_op jit(solution)/shard_map/ppermute | solution.py:216
  27.3 51.1 %collective-permute-start.8 = (bf16[4,128,2048]{2,1,0:T(8,128)(2,1)}, bf16[4,128,2048]{2,1,0:T(8,128)(2,1)}, u32[]{:S(2)}, u32[]{:S(2)}) collective-permute-start(bf16[4,128,2048]{2,1,0:T(8,128)(2,1)} %collective-permute-done.7.refs_3_), channel_id=1, source_target_pairs={{0,8},{8,0},{1,9},{9,1},{2,10},{10,2},{3,11},{11,3},{4,12},{12,4},... | collective-permute-start | bytes 6291464 | tf_op jit(solution)/shard_map/ppermute | solution.py:235
  29.6 16.0 %collective-permute-start.2 = (bf16[128,2048]{1,0:T(8,128)(2,1)}, bf16[128,2048]{1,0:T(8,128)(2,1)S(1)}, u32[]{:S(2)}, u32[]{:S(2)}) collective-permute-start(bf16[128,2048]{1,0:T(8,128)(2,1)} %refs_8_.1), channel_id=1, source_target_pairs={{0,224},{32,0},{64,32},{96,64},{128,96},{160,128},{192,160},{224,1... | collective-permute-start | bytes 1572872 | tf_op jit(solution)/shard_map/ppermute | solution.py:217
  34.0 15.6 %collective-permute-start.4 = (bf16[64,2048]{1,0:T(8,128)(2,1)S(1)}, bf16[64,2048]{1,0:T(8,128)(2,1)S(1)}, u32[]{:S(2)}, u32[]{:S(2)}) collective-permute-start(bf16[64,2048]{1,0:T(8,128)(2,1)S(1)} %get-tuple-element.35), channel_id=1, source_target_pairs={{0,32},{32,64},{64,96},{96,128},{128,160},{160,192},{192,224},{224... | collective-permute-start | bytes 786440 | tf_op jit(solution)/shard_map/ppermute | solution.py:216
  34.1 15.5 %collective-permute-start.3 = (bf16[64,2048]{1,0:T(8,128)(2,1)S(1)}, bf16[64,2048]{1,0:T(8,128)(2,1)}, u32[]{:S(2)}, u32[]{:S(2)}) collective-permute-start(bf16[64,2048]{1,0:T(8,128)(2,1)S(1)} %get-tuple-element.36), channel_id=1, source_target_pairs={{0,32},{32,64},{64,96},{96,128},{128,160},{160,192},{192,224},{224... | collective-permute-start | bytes 786440 | tf_op jit(solution)/shard_map/ppermute | solution.py:216
  46.3 8.1 %collective-permute-start.6 = (bf16[64,2048]{1,0:T(8,128)(2,1)S(1)}, bf16[64,2048]{1,0:T(8,128)(2,1)}, u32[]{:S(2)}, u32[]{:S(2)}) collective-permute-start(bf16[64,2048]{1,0:T(8,128)(2,1)S(1)} %get-tuple-element.33), channel_id=1, source_target_pairs={{0,224},{32,0},{64,32},{96,64},{128,96},{160,128},{192,160},{224,1... | collective-permute-start | bytes 786440 | tf_op jit(solution)/shard_map/ppermute | solution.py:217
  49.6 10.5 %collective-permute-start.5 = (bf16[64,2048]{1,0:T(8,128)(2,1)}, bf16[64,2048]{1,0:T(8,128)(2,1)}, u32[]{:S(2)}, u32[]{:S(2)}) collective-permute-start(bf16[64,2048]{1,0:T(8,128)(2,1)} %get-tuple-element.34), channel_id=1, source_target_pairs={{0,224},{32,0},{64,32},{96,64},{128,96},{160,128},{192,160},{224,1... | collective-permute-start | bytes 786440 | tf_op jit(solution)/shard_map/ppermute | solution.py:217
  49.6 10.5 %collective-permute-start.9 = (bf16[64,2048]{1,0:T(8,128)(2,1)}, bf16[64,2048]{1,0:T(8,128)(2,1)}, u32[]{:S(2)}, u32[]{:S(2)}) collective-permute-start(bf16[64,2048]{1,0:T(8,128)(2,1)} %collective-permute-done.3.refs_4_.refs_6_), channel_id=1, source_target_pairs={{0,32},{32,64},{64,96},{96,128},{128,160},{160,192},{192,224},{224... | collective-permute-start | bytes 786440 | tf_op jit(solution)/shard_map/ppermute | solution.py:216
  54.4 11.3 %collective-permute-start.12 = (bf16[64,2048]{1,0:T(8,128)(2,1)}, bf16[64,2048]{1,0:T(8,128)(2,1)}, u32[]{:S(2)}, u32[]{:S(2)}) collective-permute-start(bf16[64,2048]{1,0:T(8,128)(2,1)} %collective-permute-done.6.refs_7_.refs_9_), channel_id=1, source_target_pairs={{0,224},{32,0},{64,32},{96,64},{128,96},{160,128},{192,160},{224,1... | collective-permute-start | bytes 786440 | tf_op jit(solution)/shard_map/ppermute | solution.py:217
  60.1 23.4 %collective-permute-start.10 = (bf16[64,2048]{1,0:T(8,128)(2,1)S(1)}, bf16[64,2048]{1,0:T(8,128)(2,1)S(1)}, u32[]{:S(2)}, u32[]{:S(2)}) collective-permute-start(bf16[64,2048]{1,0:T(8,128)(2,1)S(1)} %collective-permute-done.4.refs_5_.refs_7_), channel_id=1, source_target_pairs={{0,32},{32,64},{64,96},{96,128},{128,160},{160,192},{192,224},{224... | collective-permute-start | bytes 786440 | tf_op jit(solution)/shard_map/ppermute | solution.py:216
  60.1 23.4 %collective-permute-start.11 = (bf16[64,2048]{1,0:T(8,128)(2,1)}, bf16[64,2048]{1,0:T(8,128)(2,1)S(1)}, u32[]{:S(2)}, u32[]{:S(2)}) collective-permute-start(bf16[64,2048]{1,0:T(8,128)(2,1)} %collective-permute-done.5.refs_6_.refs_8_), channel_id=1, source_target_pairs={{0,224},{32,0},{64,32},{96,64},{128,96},{160,128},{192,160},{224,1... | collective-permute-start | bytes 786440 | tf_op jit(solution)/shard_map/ppermute | solution.py:217
  65.8 22.7 %collective-permute-start.13 = (bf16[64,2048]{1,0:T(8,128)(2,1)}, bf16[64,2048]{1,0:T(8,128)(2,1)S(1)}, u32[]{:S(2)}, u32[]{:S(2)}) collective-permute-start(bf16[64,2048]{1,0:T(8,128)(2,1)} %collective-permute-done.9.refs_6_), channel_id=1, source_target_pairs={{0,32},{32,64},{64,96},{96,128},{128,160},{160,192},{192,224},{224... | collective-permute-start | bytes 786440 | tf_op jit(solution)/shard_map/ppermute | solution.py:241
  65.8 22.7 %collective-permute-start.14 = (bf16[64,2048]{1,0:T(8,128)(2,1)}, bf16[64,2048]{1,0:T(8,128)(2,1)S(1)}, u32[]{:S(2)}, u32[]{:S(2)}) collective-permute-start(bf16[64,2048]{1,0:T(8,128)(2,1)} %collective-permute-done.12.refs_9_), channel_id=1, source_target_pairs={{0,224},{32,0},{64,32},{96,64},{128,96},{160,128},{192,160},{224,1... | collective-permute-start | bytes 786440 | tf_op jit(solution)/shard_map/ppermute | solution.py:243
  69.2 1.0 copy-start
  83.6 4.9 %copy-start.1 = (bf16[128,2048]{1,0:T(8,128)(2,1)S(1)}, bf16[128,2048]{1,0:T(8,128)(2,1)}, u32[]{:S(2)}) copy-start(bf16[128,2048]{1,0:T(8,128)(2,1)} %refs_8_.1) | copy-start | bytes 1572868
  88.4 22.4 %copy-start.3 = (s32[4,4]{1,0:T(4,128)S(1)}, s32[4,4]{1,0:T(4,128)}, u32[]{:S(2)}) copy-start(s32[4,4]{1,0:T(4,128)} %param.6) | copy-start | bytes 196

commit v4 on v3

--- a/solution.py
+++ b/solution.py
@@ -110,12 +110,15 @@
                 out[n, 2:3, lanes] = target_logit
                 continue
             for ref in before:
-                earlier, raised = ref[n, 0:1, lanes], jnp.maximum(highest, ref[n, 0:1, lanes])
-                summed = summed * jnp.exp(highest - raised) + ref[n, 1:2, lanes] * jnp.exp(
+                m = n if ref.shape[0] == 4 else n - (2 if ref is before[-2] else 0)
+                if not 0 <= m < ref.shape[0]:
+                    continue
+                earlier, raised = ref[m, 0:1, lanes], jnp.maximum(highest, ref[m, 0:1, lanes])
+                summed = summed * jnp.exp(highest - raised) + ref[m, 1:2, lanes] * jnp.exp(
                     earlier - raised
                 )
                 highest = raised
-                target_logit = target_logit + ref[n, 2:3, lanes]
+                target_logit = target_logit + ref[m, 2:3, lanes]
             total, message = highest + jnp.log(summed), []
             left = lax.broadcasted_iota(jnp.int32, (1, 128), 1) < 64
             for k in range(2):
@@ -244,12 +247,11 @@
     early = gathered[1] + gathered[2]
     (wanted_far,) = after((wanted,), (near_found,))
     far_found, far = score_blocks({(3,): diagonal}, {2: across}, [3, 2], early, first, wanted_far)
-    found = jnp.concatenate([near_found, far_found])
     stores, every = held | {(2,): far, (3,): diagonal}, [0, 1, 2, 3]
     (latter,) = score_blocks(stores, {}, every, gathered[3], first, wanted_far)
     (wanted_last,) = after((wanted,), (latter,))
     (message,) = score_blocks(
-        stores, {}, every, gathered[0] + last, first, wanted_last, (found, latter), (0,)
+        stores, {}, every, gathered[0] + last, first, wanted_last, (near_found, far_found, latter), (0,)
     )
     message = message.reshape(32, 1, 128)
     received = lax.all_to_all(

time: 124 us -> 115 us (0.927)
  waiting for transfers between devices: 40.2 us -> 32.8 us
  starting transfers between devices: 28.1 us -> 24.8 us
    ppermute x5, waiting for transfers between devices: 19 us -> 7.22 us  [forward(): down[k] = lax.ppermute(down[k], 'z', around(8, -1))]
    ppermute x5, waiting for transfers between devices: 0.01 us -> 8.36 us  [forward(): up[k] = lax.ppermute(up[k], 'z', around(8, 1))]
    ppermute x1, waiting for transfers between devices: 21.1 us -> 17.2 us  [per_device(): across = lax.ppermute(hidden, ('yl', 'c', 'yh'), across_y())]
    all_to_all x1, blocking collectives: 12 us -> 13.5 us  [per_device(): lax.all_to_all(copies, ('z', 'yl', 'c'), split_axis=0, concat_axis=0, til...]
    ppermute x5, starting transfers between devices: 14.7 us -> 13.2 us  [forward(): down[k] = lax.ppermute(down[k], 'z', around(8, -1))]
  transfers between devices with their start and end apart: 15 -> 15, of which waited for: 5 -> 5; matrix products, arithmetic and copies ran while one was open for 1% -> 1% of each run, Pallas kernels for 15% -> 16%
where the time goes in v4:
time: 115 us
  waiting for transfers between devices  32.8 us (29%)
  blocking collectives  30.7 us (27%)
  starting transfers between devices  24.8 us (22%)
  Pallas kernels  23.2 us (20%)
  local copies, waits for them, and re-layouts  2.02 us (2%)
  other arithmetic  1.18 us (1%)
    pallas_call x6, Pallas kernels, score_blocks(): pl.pallas_call(functools.partial(scores_kernel, done_near, len(before), l...  23.1 us
    all_to_all x1, blocking collectives, per_device(): lax.all_to_all(message, ('yl', 'c', 'yh', 'x'), split_axis=0, concat_axis...  17.2 us
    ppermute x1, waiting for transfers between devices, per_device(): across = lax.ppermute(hidden, ('yl', 'c', 'yh'), across_y())  17.2 us
    all_to_all x1, blocking collectives, per_device(): lax.all_to_all(copies, ('z', 'yl', 'c'), split_axis=0, concat_axis=0, til...  13.5 us
    ppermute x5, starting transfers between devices, forward(): down[k] = lax.ppermute(down[k], 'z', around(8, -1))  13.2 us
    ppermute x5, waiting for transfers between devices, forward(): up[k] = lax.ppermute(up[k], 'z', around(8, 1))  8.36 us
    ppermute x5, waiting for transfers between devices, forward(): down[k] = lax.ppermute(down[k], 'z', around(8, -1))  7.22 us
    ppermute x1, starting transfers between devices, per_device(): last.append((lax.ppermute(down[k], 'z', around(8, -1)), PARTS * 4 + k))  2.67 us
  transfers between devices with their start and end apart: 15, of which 5 were waited for; matrix products, arithmetic and copies ran while one was open for 1% of the time, Pallas kernels for 16%

profile of v4, /device:TPU:1, one launch (start us, length us, event | category | flops | bytes accessed | tf_op | source)
XLA Modules:
  0.0 114.9 jit_solution(12342403440472014594)
XLA Ops:
  0.0 2.1 %collective-permute-start.7 = (bf16[4,128,2048]{2,1,0:T(8,128)(2,1)}, bf16[4,128,2048]{2,1,0:T(8,128)(2,1)}, u32[]{:S(2)}, u32[]{:S(2)}) collective-permute-start(bf16[4,128,2048]{2,1,0:T(8,128)(2,1)} %refs_3_.1), channel_id=1, source_target_pairs={{0,20},{8,24},{16,0},{24,12},{4,16},{12,28},{20,4},{28,8},{1,21},{... | collective-permute-start | bytes 6291464 | tf_op jit(solution)/shard_map/ppermute | solution.py:228
  2.1 2.4 %collective-permute-start = (bf16[4,128,2048]{2,1,0:T(8,128)(2,1)}, bf16[4,128,2048]{2,1,0:T(8,128)(2,1)S(1)}, u32[]{:S(2)}, u32[]{:S(2)}) collective-permute-start(bf16[4,128,2048]{2,1,0:T(8,128)(2,1)} %refs_3_.1), channel_id=1, source_target_pairs={{0,8},{8,0},{1,9},{9,1},{2,10},{10,2},{3,11},{11,3},{4,12},{12,4},... | collective-permute-start | bytes 6291464 | tf_op jit(solution)/shard_map/ppermute | solution.py:227
  4.5 1.6 %collective-permute-start.1 = (bf16[128,2048]{1,0:T(8,128)(2,1)}, bf16[128,2048]{1,0:T(8,128)(2,1)S(1)}, u32[]{:S(2)}, u32[]{:S(2)}) collective-permute-start(bf16[128,2048]{1,0:T(8,128)(2,1)} %refs_9_.1), channel_id=1, source_target_pairs={{0,32},{32,64},{64,96},{96,128},{128,160},{160,192},{192,224},{224... | collective-permute-start | bytes 1572872 | tf_op jit(solution)/shard_map/ppermute | solution.py:219
  6.1 3.9 %collective-permute-start.2 = (bf16[128,2048]{1,0:T(8,128)(2,1)}, bf16[128,2048]{1,0:T(8,128)(2,1)S(1)}, u32[]{:S(2)}, u32[]{:S(2)}) collective-permute-start(bf16[128,2048]{1,0:T(8,128)(2,1)} %refs_9_.1), channel_id=1, source_target_pairs={{0,224},{32,0},{64,32},{96,64},{128,96},{160,128},{192,160},{224,1... | collective-permute-start | bytes 1572872 | tf_op jit(solution)/shard_map/ppermute | solution.py:220
  10.1 17.2 %collective-permute-done.7.refs_3_ = bf16[4,128,2048]{2,1,0:T(8,128)(2,1)} collective-permute-done((bf16[4,128,2048]{2,1,0:T(8,128)(2,1)}, bf16[4,128,2048]{2,1,0:T(8,128)(2,1)}, u32[]{:S(2)}, u32[]{:S(2)}) %collective-permute-start.7) | collective-permute-done | bytes 2097184 | tf_op jit(solution)/shard_map/ppermute | solution.py:228
  27.3 2.3 %collective-permute-start.8 = (bf16[4,128,2048]{2,1,0:T(8,128)(2,1)}, bf16[4,128,2048]{2,1,0:T(8,128)(2,1)}, u32[]{:S(2)}, u32[]{:S(2)}) collective-permute-start(bf16[4,128,2048]{2,1,0:T(8,128)(2,1)} %collective-permute-done.7.refs_3_), channel_id=1, source_target_pairs={{0,8},{8,0},{1,9},{9,1},{2,10},{10,2},{3,11},{11,3},{4,12},{12,4},... | collective-permute-start | bytes 6291464 | tf_op jit(solution)/shard_map/ppermute | solution.py:238
  29.6 0.0 collective-permute-done.1.refs_4_
  29.6 0.5 collective-permute-start.3
  30.1 0.0 collective-permute-done.2.refs_5_
  30.1 0.8 fusion.14
  30.9 4.0 %collective-permute-start.6 = (bf16[64,2048]{1,0:T(8,128)(2,1)S(1)}, bf16[64,2048]{1,0:T(8,128)(2,1)}, u32[]{:S(2)}, u32[]{:S(2)}) collective-permute-start(bf16[64,2048]{1,0:T(8,128)(2,1)S(1)} %get-tuple-element.33), channel_id=1, source_target_pairs={{0,224},{32,0},{64,32},{96,64},{128,96},{160,128},{192,160},{224,1... | collective-permute-start | bytes 786440 | tf_op jit(solution)/shard_map/ppermute | solution.py:220
  34.9 0.0 collective-permute-start.4
  34.9 5.9 %collective-permute-done.3.refs_4_.refs_6_ = bf16[64,2048]{1,0:T(8,128)(2,1)S(1)} collective-permute-done((bf16[64,2048]{1,0:T(8,128)(2,1)S(1)}, bf16[64,2048]{1,0:T(8,128)(2,1)S(1)}, u32[]{:S(2)}, u32[]{:S(2)}) %collective-permute-start.3) | collective-permute-done | bytes 262176 | tf_op jit(solution)/shard_map/ppermute | solution.py:219
  40.8 1.3 %collective-permute-start.5 = (bf16[64,2048]{1,0:T(8,128)(2,1)}, bf16[64,2048]{1,0:T(8,128)(2,1)}, u32[]{:S(2)}, u32[]{:S(2)}) collective-permute-start(bf16[64,2048]{1,0:T(8,128)(2,1)} %get-tuple-element.34), channel_id=1, source_target_pairs={{0,224},{32,0},{64,32},{96,64},{128,96},{160,128},{192,160},{224,1... | collective-permute-start | bytes 786440 | tf_op jit(solution)/shard_map/ppermute | solution.py:220
  42.1 0.0 collective-permute-done.6.refs_7_.refs_9_
  42.1 2.0 %collective-permute-start.12 = (bf16[64,2048]{1,0:T(8,128)(2,1)}, bf16[64,2048]{1,0:T(8,128)(2,1)}, u32[]{:S(2)}, u32[]{:S(2)}) collective-permute-start(bf16[64,2048]{1,0:T(8,128)(2,1)} %collective-permute-done.6.refs_7_.refs_9_), channel_id=1, source_target_pairs={{0,224},{32,0},{64,32},{96,64},{128,96},{160,128},{192,160},{224,1... | collective-permute-start | bytes 786440 | tf_op jit(solution)/shard_map/ppermute | solution.py:220
  44.0 2.4 %collective-permute-done.4.refs_5_.refs_7_ = bf16[64,2048]{1,0:T(8,128)(2,1)} collective-permute-done((bf16[64,2048]{1,0:T(8,128)(2,1)S(1)}, bf16[64,2048]{1,0:T(8,128)(2,1)}, u32[]{:S(2)}, u32[]{:S(2)}) %collective-permute-start.4) | collective-permute-done | bytes 262176 | tf_op jit(solution)/shard_map/ppermute | solution.py:219
  46.5 0.0 collective-permute-start.9
  46.5 0.1 shard_map.46.refs_1_
  46.6 1.6 %collective-permute-done.5.refs_6_.refs_8_ = bf16[64,2048]{1,0:T(8,128)(2,1)} collective-permute-done((bf16[64,2048]{1,0:T(8,128)(2,1)}, bf16[64,2048]{1,0:T(8,128)(2,1)}, u32[]{:S(2)}, u32[]{:S(2)}) %collective-permute-start.5) | collective-permute-done | bytes 262176 | tf_op jit(solution)/shard_map/ppermute | solution.py:220
  48.2 0.0 collective-permute-start.10
  48.2 5.6 %collective-permute-done.12.refs_9_ = bf16[64,2048]{1,0:T(8,128)(2,1)} collective-permute-done((bf16[64,2048]{1,0:T(8,128)(2,1)}, bf16[64,2048]{1,0:T(8,128)(2,1)}, u32[]{:S(2)}, u32[]{:S(2)}) %collective-permute-start.12) | collective-permute-done | bytes 262176 | tf_op jit(solution)/shard_map/ppermute | solution.py:220
  53.8 2.0 %collective-permute-start.11 = (bf16[64,2048]{1,0:T(8,128)(2,1)}, bf16[64,2048]{1,0:T(8,128)(2,1)S(1)}, u32[]{:S(2)}, u32[]{:S(2)}) collective-permute-start(bf16[64,2048]{1,0:T(8,128)(2,1)} %collective-permute-done.5.refs_6_.refs_8_), channel_id=1, source_target_pairs={{0,224},{32,0},{64,32},{96,64},{128,96},{160,128},{192,160},{224,1... | collective-permute-start | bytes 786440 | tf_op jit(solution)/shard_map/ppermute | solution.py:220
  55.8 0.0 collective-permute-done.9.refs_6_
  55.8 0.0 collective-permute-start.13
  55.8 0.0 collective-permute-done.refs_2_.refs_3_.refs_6_
  55.9 2.7 %collective-permute-start.14 = (bf16[64,2048]{1,0:T(8,128)(2,1)}, bf16[64,2048]{1,0:T(8,128)(2,1)S(1)}, u32[]{:S(2)}, u32[]{:S(2)}) collective-permute-start(bf16[64,2048]{1,0:T(8,128)(2,1)} %collective-permute-done.12.refs_9_), channel_id=1, source_target_pairs={{0,224},{32,0},{64,32},{96,64},{128,96},{160,128},{192,160},{224,1... | collective-permute-start | bytes 786440 | tf_op jit(solution)/shard_map/ppermute | solution.py:246
  58.5 1.0 copy-done
  59.6 3.3 %shard_map.47 = (f32[2,3,512]{2,1,0:T(4,128)S(1)}, bf16[1,4,128,2048]{3,2,1,0:T(8,128)(2,1)S(1)}) custom-call(s32[17]{0:T(128)S(1)} %compare_select_fusion.refs_0_, s32[1,512]{1,0:T(1,128)S(1)} %shard_map.46.refs_1_, bf16[4,128,2048]{2,1,0:T(8,128)(2,1)S(1)} %collective-permute-done.refs_2_.refs_3_.refs_6_, bf16[4,128,2048]{2,1,0:T(8,128)(2,1)} %refs_3_.1, ...), custom_call_target="tpu_custom_call" | custom-call | flops 536870912 | bytes 4718592 | tf_op jit(solution)/shard_map/pallas_call | solution.py:140
  62.9 2.7 %shard_map.49 = f32[2,3,512]{2,1,0:T(4,128)S(1)} custom-call(s32[17]{0:T(128)S(1)} %compare_select_fusion.refs_0_, s32[1,512]{1,0:T(1,128)S(1)} %shard_map.46.refs_1_, bf16[1,4,128,2048]{3,2,1,0:T(8,128)(2,1)S(1)} %get-tuple-element.18.refs_2_.refs_5_, bf16[4,128,2048]{2,1,0:T(8,128)(2,1)S(1)} %collective-permute-done.refs_2_.refs_3_.refs_6_, ...), custom_call_target="tpu_custom_call" | custom-call | flops 1073741824 | bytes 5242880 | tf_op jit(solution)/shard_map/pallas_call | solution.py:140
  65.6 2.1 %shard_map.48 = f32[2,3,512]{2,1,0:T(4,128)S(1)} custom-call(s32[17]{0:T(128)S(1)} %compare_select_fusion.refs_0_, s32[1,512]{1,0:T(1,128)S(1)} %shard_map.46.refs_1_, bf16[1,4,128,2048]{3,2,1,0:T(8,128)(2,1)S(1)} %get-tuple-element.18.refs_2_.refs_5_, bf16[4,128,2048]{2,1,0:T(8,128)(2,1)S(1)} %collective-permute-done.refs_2_.refs_3_.refs_6_, ...), custom_call_target="tpu_custom_call" | custom-call | flops 1073741824 | bytes 5242880 | tf_op jit(solution)/shard_map/pallas_call | solution.py:140
  67.8 0.0 collective-permute-done.8.refs_2_.refs_5_.refs_8_
  67.8 5.5 %shard_map.50 = (f32[2,3,512]{2,1,0:T(4,128)S(1)}, bf16[1,4,128,2048]{3,2,1,0:T(8,128)(2,1)S(1)}) custom-call(s32[17]{0:T(128)S(1)} %compare_select_fusion.refs_0_, s32[1,512]{1,0:T(1,128)S(1)} %shard_map.46.refs_1_, bf16[4,128,2048]{2,1,0:T(8,128)(2,1)} %collective-permute-done.8.refs_2_.refs_5_.refs_8_, ...), custom_call_target="tpu_custom_call" | custom-call | flops 2147483648 | bytes 6291456 | tf_op jit(solution)/shard_map/pallas_call | solution.py:140
  73.3 0.0 collective-permute-done.10.refs_7_
  73.3 0.0 copy-start.1
  73.3 4.8 %shard_map.51.refs_4_ = f32[4,3,512]{2,1,0:T(4,128)S(1)} custom-call(s32[17]{0:T(128)S(1)} %compare_select_fusion.refs_0_, s32[1,512]{1,0:T(1,128)S(1)} %shard_map.46.refs_1_, bf16[1,4,128,2048]{3,2,1,0:T(8,128)(2,1)S(1)} %get-tuple-element.18.refs_2_.refs_5_, bf16[4,128,2048]{2,1,0:T(8,128)(2,1)S(1)} %collective-permute-done.refs_2_.refs_3_.refs_6_, ...), custom_call_target="tpu_custom_call" | custom-call | flops 2147483648 | bytes 9437184 | tf_op jit(solution)/shard_map/pallas_call | solution.py:140
  78.1 0.0 collective-permute-done.14.refs_11_
  78.1 0.0 copy-start.3
  78.1 4.7 %shard_map.52 = f32[4,8,128]{2,1,0:T(8,128)S(1)} custom-call(s32[17]{0:T(128)S(1)} %compare_select_fusion.refs_0_, s32[1,512]{1,0:T(1,128)S(1)} %shard_map.46.refs_1_, f32[2,3,512]{2,1,0:T(4,128)S(1)} %pad_maximum_fusion.refs_2_, f32[2,3,512]{2,1,0:T(4,128)S(1)} %get-tuple-element.22.refs_3_, f32[4,3,512]{2,1,0:T(4,128)S(1)} %shard_map.51.refs_4_, ...), custom_call_target="tpu_custom_call" | custom-call | flops 2147483648 | bytes 9437184 | tf_op jit(solution)/shard_map/pallas_call | solution.py:140
  82.9 17.2 %all_to_all.10 = f32[32,1,128]{2,1,0:T(1,128)S(1)} all-to-all(f32[32,1,128]{2,1,0:T(1,128)S(1)} %bitcast.9), channel_id=1, replica_groups=mesh['z'=8,'yl'=2,'c'=2,'yh'=2,'x'=4] {'yl','c','yh','x'}, dimensions={0} | all-to-all | bytes 32768 | tf_op jit(solution)/shard_map/all_to_all | solution.py:257
  100.2 0.1 select_reduce_fusion
  100.3 0.1 exponential_reduce_fusion
  100.4 0.1 sub.103
  100.5 0.1 fusion.13
  100.6 0.1 pad_maximum_fusion.1
  100.7 13.5 %all_to_all.11 = f32[32,1,32]{2,1,0:T(1,128)S(1)} all-to-all(f32[32,1,32]{2,1,0:T(1,128)S(1)} %broadcast_in_dim.22), channel_id=1, replica_groups=mesh['z'=8,'yl'=2,'c'=2,'yh'=2,'x'=4] {'z','yl','c'}, dimensions={0} | all-to-all | bytes 8192 | tf_op jit(solution)/shard_map/all_to_all | solution.py:276
  114.2 0.1 fusion.16
  114.3 0.7 rsqrt_multiply_fusion
  (18 shorter events, 0.2 us)
Async XLA Ops:
  0.0 46.5 %copy-start.2 = (s32[128]{0:T(128)S(1)}, s32[128]{0:T(128)}, u32[]{:S(2)}) copy-start(s32[128]{0:T(128)} %param.5) | copy-start | bytes 1540
  0.0 27.3 %collective-permute-start.7 = (bf16[4,128,2048]{2,1,0:T(8,128)(2,1)}, bf16[4,128,2048]{2,1,0:T(8,128)(2,1)}, u32[]{:S(2)}, u32[]{:S(2)}) collective-permute-start(bf16[4,128,2048]{2,1,0:T(8,128)(2,1)} %refs_3_.1), channel_id=1, source_target_pairs={{0,20},{8,24},{16,0},{24,12},{4,16},{12,28},{20,4},{28,8},{1,21},{... | collective-permute-start | bytes 6291464 | tf_op jit(solution)/shard_map/ppermute | solution.py:228
  2.1 53.7 %collective-permute-start = (bf16[4,128,2048]{2,1,0:T(8,128)(2,1)}, bf16[4,128,2048]{2,1,0:T(8,128)(2,1)S(1)}, u32[]{:S(2)}, u32[]{:S(2)}) collective-permute-start(bf16[4,128,2048]{2,1,0:T(8,128)(2,1)} %refs_3_.1), channel_id=1, source_target_pairs={{0,8},{8,0},{1,9},{9,1},{2,10},{10,2},{3,11},{11,3},{4,12},{12,4},... | collective-permute-start | bytes 6291464 | tf_op jit(solution)/shard_map/ppermute | solution.py:227
  4.5 25.0 %collective-permute-start.1 = (bf16[128,2048]{1,0:T(8,128)(2,1)}, bf16[128,2048]{1,0:T(8,128)(2,1)S(1)}, u32[]{:S(2)}, u32[]{:S(2)}) collective-permute-start(bf16[128,2048]{1,0:T(8,128)(2,1)} %refs_9_.1), channel_id=1, source_target_pairs={{0,32},{32,64},{64,96},{96,128},{128,160},{160,192},{192,224},{224... | collective-permute-start | bytes 1572872 | tf_op jit(solution)/shard_map/ppermute | solution.py:219
  6.1 24.0 %collective-permute-start.2 = (bf16[128,2048]{1,0:T(8,128)(2,1)}, bf16[128,2048]{1,0:T(8,128)(2,1)S(1)}, u32[]{:S(2)}, u32[]{:S(2)}) collective-permute-start(bf16[128,2048]{1,0:T(8,128)(2,1)} %refs_9_.1), channel_id=1, source_target_pairs={{0,224},{32,0},{64,32},{96,64},{128,96},{160,128},{192,160},{224,1... | collective-permute-start | bytes 1572872 | tf_op jit(solution)/shard_map/ppermute | solution.py:220
  27.3 40.5 %collective-permute-start.8 = (bf16[4,128,2048]{2,1,0:T(8,128)(2,1)}, bf16[4,128,2048]{2,1,0:T(8,128)(2,1)}, u32[]{:S(2)}, u32[]{:S(2)}) collective-permute-start(bf16[4,128,2048]{2,1,0:T(8,128)(2,1)} %collective-permute-done.7.refs_3_), channel_id=1, source_target_pairs={{0,8},{8,0},{1,9},{9,1},{2,10},{10,2},{3,11},{11,3},{4,12},{12,4},... | collective-permute-start | bytes 6291464 | tf_op jit(solution)/shard_map/ppermute | solution.py:238
  29.6 11.2 %collective-permute-start.3 = (bf16[64,2048]{1,0:T(8,128)(2,1)S(1)}, bf16[64,2048]{1,0:T(8,128)(2,1)S(1)}, u32[]{:S(2)}, u32[]{:S(2)}) collective-permute-start(bf16[64,2048]{1,0:T(8,128)(2,1)S(1)} %get-tuple-element.36), channel_id=1, source_target_pairs={{0,32},{32,64},{64,96},{96,128},{128,160},{160,192},{192,224},{224... | collective-permute-start | bytes 786440 | tf_op jit(solution)/shard_map/ppermute | solution.py:219
  30.9 11.2 %collective-permute-start.6 = (bf16[64,2048]{1,0:T(8,128)(2,1)S(1)}, bf16[64,2048]{1,0:T(8,128)(2,1)}, u32[]{:S(2)}, u32[]{:S(2)}) collective-permute-start(bf16[64,2048]{1,0:T(8,128)(2,1)S(1)} %get-tuple-element.33), channel_id=1, source_target_pairs={{0,224},{32,0},{64,32},{96,64},{128,96},{160,128},{192,160},{224,1... | collective-permute-start | bytes 786440 | tf_op jit(solution)/shard_map/ppermute | solution.py:220
  34.9 11.6 %collective-permute-start.4 = (bf16[64,2048]{1,0:T(8,128)(2,1)S(1)}, bf16[64,2048]{1,0:T(8,128)(2,1)}, u32[]{:S(2)}, u32[]{:S(2)}) collective-permute-start(bf16[64,2048]{1,0:T(8,128)(2,1)S(1)} %get-tuple-element.35), channel_id=1, source_target_pairs={{0,32},{32,64},{64,96},{96,128},{128,160},{160,192},{192,224},{224... | collective-permute-start | bytes 786440 | tf_op jit(solution)/shard_map/ppermute | solution.py:219
  40.8 7.4 %collective-permute-start.5 = (bf16[64,2048]{1,0:T(8,128)(2,1)}, bf16[64,2048]{1,0:T(8,128)(2,1)}, u32[]{:S(2)}, u32[]{:S(2)}) collective-permute-start(bf16[64,2048]{1,0:T(8,128)(2,1)} %get-tuple-element.34), channel_id=1, source_target_pairs={{0,224},{32,0},{64,32},{96,64},{128,96},{160,128},{192,160},{224,1... | collective-permute-start | bytes 786440 | tf_op jit(solution)/shard_map/ppermute | solution.py:220
  42.1 11.7 %collective-permute-start.12 = (bf16[64,2048]{1,0:T(8,128)(2,1)}, bf16[64,2048]{1,0:T(8,128)(2,1)}, u32[]{:S(2)}, u32[]{:S(2)}) collective-permute-start(bf16[64,2048]{1,0:T(8,128)(2,1)} %collective-permute-done.6.refs_7_.refs_9_), channel_id=1, source_target_pairs={{0,224},{32,0},{64,32},{96,64},{128,96},{160,128},{192,160},{224,1... | collective-permute-start | bytes 786440 | tf_op jit(solution)/shard_map/ppermute | solution.py:220
  46.5 9.4 %collective-permute-start.9 = (bf16[64,2048]{1,0:T(8,128)(2,1)S(1)}, bf16[64,2048]{1,0:T(8,128)(2,1)}, u32[]{:S(2)}, u32[]{:S(2)}) collective-permute-start(bf16[64,2048]{1,0:T(8,128)(2,1)S(1)} %collective-permute-done.3.refs_4_.refs_6_), channel_id=1, source_target_pairs={{0,32},{32,64},{64,96},{96,128},{128,160},{160,192},{192,224},{224... | collective-permute-start | bytes 786440 | tf_op jit(solution)/shard_map/ppermute | solution.py:219
  48.2 25.1 %collective-permute-start.10 = (bf16[64,2048]{1,0:T(8,128)(2,1)}, bf16[64,2048]{1,0:T(8,128)(2,1)S(1)}, u32[]{:S(2)}, u32[]{:S(2)}) collective-permute-start(bf16[64,2048]{1,0:T(8,128)(2,1)} %collective-permute-done.4.refs_5_.refs_7_), channel_id=1, source_target_pairs={{0,32},{32,64},{64,96},{96,128},{128,160},{160,192},{192,224},{224... | collective-permute-start | bytes 786440 | tf_op jit(solution)/shard_map/ppermute | solution.py:219
  53.8 19.5 %collective-permute-start.11 = (bf16[64,2048]{1,0:T(8,128)(2,1)}, bf16[64,2048]{1,0:T(8,128)(2,1)S(1)}, u32[]{:S(2)}, u32[]{:S(2)}) collective-permute-start(bf16[64,2048]{1,0:T(8,128)(2,1)} %collective-permute-done.5.refs_6_.refs_8_), channel_id=1, source_target_pairs={{0,224},{32,0},{64,32},{96,64},{128,96},{160,128},{192,160},{224,1... | collective-permute-start | bytes 786440 | tf_op jit(solution)/shard_map/ppermute | solution.py:220
  55.8 22.3 %collective-permute-start.13 = (bf16[64,2048]{1,0:T(8,128)(2,1)}, bf16[64,2048]{1,0:T(8,128)(2,1)S(1)}, u32[]{:S(2)}, u32[]{:S(2)}) collective-permute-start(bf16[64,2048]{1,0:T(8,128)(2,1)} %collective-permute-done.9.refs_6_), channel_id=1, source_target_pairs={{0,32},{32,64},{64,96},{96,128},{128,160},{160,192},{192,224},{224... | collective-permute-start | bytes 786440 | tf_op jit(solution)/shard_map/ppermute | solution.py:244
  55.9 22.3 %collective-permute-start.14 = (bf16[64,2048]{1,0:T(8,128)(2,1)}, bf16[64,2048]{1,0:T(8,128)(2,1)S(1)}, u32[]{:S(2)}, u32[]{:S(2)}) collective-permute-start(bf16[64,2048]{1,0:T(8,128)(2,1)} %collective-permute-done.12.refs_9_), channel_id=1, source_target_pairs={{0,224},{32,0},{64,32},{96,64},{128,96},{160,128},{192,160},{224,1... | collective-permute-start | bytes 786440 | tf_op jit(solution)/shard_map/ppermute | solution.py:246
  58.5 1.0 copy-start
  73.3 4.8 %copy-start.1 = (bf16[128,2048]{1,0:T(8,128)(2,1)S(1)}, bf16[128,2048]{1,0:T(8,128)(2,1)}, u32[]{:S(2)}) copy-start(bf16[128,2048]{1,0:T(8,128)(2,1)} %refs_9_.1) | copy-start | bytes 1572868
  78.1 22.0 %copy-start.3 = (s32[4,4]{1,0:T(4,128)S(1)}, s32[4,4]{1,0:T(4,128)}, u32[]{:S(2)}) copy-start(s32[4,4]{1,0:T(4,128)} %param.6) | copy-start | bytes 196
